TPU v7x, 256 devices: a whole 4x4x8 slice. The times are simulated.
256 devices in a mesh: row: 8 (over y, core), col: 32 (over z, x).
Axes of the slice: x: 4, y: 4, z: 8, core: 2. Of those that a mesh axis runs over, the one named last changes fastest.
Arguments:
- factor: float32 [6, 2048, 6, 2048], P(None, 'row', None, 'col'), may hold values from -0.0625 to 0.0625
- diag_inv: float32 [6, 2048, 2048], P(None, None, 'row'), may hold values from -2 to 2, as said below
- structure: int32 [6, 6, 16], P(None, None, 'row'), may hold values 0 or 1
- parent: int32 [6], replicated, may hold values from 1 to 6, as said below
- post: float32 [6, 2048, 64], P(None, 'row', 'col'), may hold values from -6 to 6
Outputs:
- mean_x: float32 [6, 2048, 64], P(None, 'row', 'col')
- variance: float32 [6, 2048], P(None, 'row')
Inputs may be any that keep to these rules, and one draw needn't show every extreme that they name: parent[s] > s for s < 5, and parent[5] = 6; every supernode has at most 2 ancestors, and some supernode has exactly that many. The diagonal of each diag_inv[s] lies in 0.5 to 2.
All inputs are finite; a program needn't handle non-finite values. No bound on the sum of `structure` on one device may be relied on, other than what follows from the above.
Results may differ from a plain program's by a relative error of at most 0.00014.
Values sent between devices are 32-bit elements; how exact they have to be, the bound alone decides.
A program may use at most 128 MiB of HBM per device.

v0:
```python
import jax
import jax.numpy as jnp
from jax import lax
from jax.sharding import Mesh
from jax.sharding import PartitionSpec as P

LEVELS = 3
COL = ("col_0", "col_1")


HIGHEST = lax.Precision.HIGHEST


def laid_out(parts, dim):
    parts = jnp.moveaxis(parts, 0, dim)
    dims = parts.shape
    return parts.reshape(*dims[:dim], dims[dim] * dims[dim + 1], *dims[dim + 2 :])


def from_everyone(array, axis):
    copies = jnp.broadcast_to(array, (lax.axis_size(axis), *array.shape))
    return lax.all_to_all(copies, axis, split_axis=0, concat_axis=0, tiled=True)


def gathered_copies(array, axis, dim):
    return laid_out(from_everyone(array, axis), dim)


def filled_up(lines, peers):
    spare = -len(lines) % peers
    return jnp.pad(lines, [(0, spare)] + [(0, 0)] * (lines.ndim - 1))


def total_of(array, axis):
    lines = array.reshape(-1, *array.shape[1:][-1:])
    padded = filled_up(lines, lax.axis_size(axis))
    own = lax.psum_scatter(padded, axis, scatter_dimension=0, tiled=True)
    whole = lax.all_gather(own, axis, axis=0, tiled=True)
    return whole[: len(lines)].reshape(array.shape)


def gathered_by_axis(array, axes, dim):
    if not axes:
        return array
    nearer = lax.all_gather(array, axes[-1], axis=dim, tiled=True)
    return gathered_by_axis(nearer, axes[:-1], dim)


def taken_together(array, axis):
    everything = from_everyone(array, axis)
    return jnp.sum(everything, axis=0)


def contract(selected, panel_piece):
    return jnp.einsum("tiw,tin->wn", panel_piece, selected, precision=HIGHEST)


def body(factor, diag_inv, structure, parent, post):
    super_count = factor.shape[0]
    row_width = factor.shape[1]
    col_width = factor.shape[3]
    full_width = diag_inv.shape[1]
    rhs_width = post.shape[2]
    row_at = lax.axis_index("row")
    col_at = lax.axis_index(COL)
    extended = jnp.concatenate([parent, jnp.full((1,), super_count, jnp.int32)])
    slot_ids = jnp.arange(super_count + 1, dtype=jnp.int32)
    targets = jnp.arange(super_count, dtype=jnp.int32)
    ancestor_hops = []
    current = parent
    for hop_index in range(super_count - 1):
        ancestor_hops.append(current)
        onehot = (current[:, None] == slot_ids[None, :]).astype(jnp.int32)
        current = jnp.sum(onehot * extended[None, :], axis=1)
    ancestry = jnp.zeros((super_count, super_count), jnp.float32)
    for hop_targets in ancestor_hops:
        ancestry = ancestry + (hop_targets[:, None] == targets[None, :]).astype(jnp.float32)
    block_rows = row_width // structure.shape[2]
    row_mask = jnp.repeat(structure.astype(jnp.float32), block_rows, axis=2) * ancestry[:, :, None]
    masked = factor * jnp.transpose(row_mask, (1, 2, 0))[:, :, :, None]
    rows_full = jnp.arange(full_width, dtype=jnp.int32)
    own_cols = row_at * row_width + jnp.arange(row_width, dtype=jnp.int32)
    lower_inv = jnp.where((rows_full[:, None] >= own_cols[None, :])[None, :, :], diag_inv, 0.0)
    unit_cols = col_at * col_width + jnp.arange(col_width, dtype=jnp.int32)
    unit_block = (rows_full[:, None] == unit_cols[None, :]).astype(jnp.float32)
    gathered = gathered_copies(post, "row", 1)
    total_cols = super_count * col_width + rhs_width
    solution = jnp.zeros((super_count, row_width, total_cols), jnp.float32)
    for current_sup in range(super_count - 1, -1, -1):
        later_cols = (current_sup + 1) * col_width
        if current_sup == super_count - 1:
            summed = jnp.zeros((full_width, rhs_width), jnp.float32)
        else:
            picks = []
            chosen_rows = []
            for slot_index in range(LEVELS - 1):
                target = ancestor_hops[slot_index][current_sup]
                is_valid = (target < super_count).astype(jnp.float32)
                clamped = jnp.minimum(target, super_count - 1)
                picks.append(
                    lax.dynamic_index_in_dim(
                        masked[:, :, current_sup, :], clamped, 0, keepdims=False
                    )
                    * is_valid
                )
                chosen_rows.append(
                    lax.dynamic_index_in_dim(solution, clamped, 0, keepdims=False)[:, later_cols:]
                )
            blocks = jnp.stack(picks)
            selected = jnp.stack(chosen_rows)
            partial_value = contract(selected, gathered_by_axis(blocks, COL, 2))
            summed = total_of(partial_value, "row")
        split_at = summed.shape[1] - rhs_width
        remaining = jnp.concatenate(
            [-summed[:, :split_at], gathered[current_sup] - summed[:, split_at:]], axis=1
        )
        right = jnp.concatenate([unit_block, remaining], axis=1)
        fresh = jnp.dot(
            lower_inv[current_sup].T, right, precision=HIGHEST, preferred_element_type=jnp.float32
        )
        solution = solution.at[current_sup, :, current_sup * col_width :].set(fresh)
    mean_x = solution[:, :, super_count * col_width :]
    unit_part = solution[:, :, : super_count * col_width]
    squares = jnp.sum(unit_part * unit_part, axis=2)
    variance = taken_together(squares, COL)
    return (mean_x, variance)


def solution(mesh):
    finer = Mesh(mesh.devices.reshape(mesh.shape["row"], 8, 4), ("row", "col_0", "col_1"))
    placed = (
        P(None, "row", None, COL),
        P(None, None, "row"),
        P(None, None, "row"),
        P(),
        P(None, "row", COL),
    )
    return jax.shard_map(
        body,
        mesh=finer,
        in_specs=placed,
        out_specs=(P(None, "row", COL), P(None, "row")),
        check_vma=False,
    )
```

profile of v0, /device:TPU:1, one launch (start us, length us, event | category | flops | bytes accessed | tf_op | source)
XLA Modules:
  0.0 674.5 jit_solution(18095809335935411941)
XLA Ops:
  7.2 1.5 fusion.93
  8.7 0.7 pad_add_fusion
  9.4 0.8 select_reduce_fusion.3
  10.4 0.6 fusion.94
  13.5 0.7 convert_element_type.106
  14.8 0.7 convert_add_fusion
  15.6 3.1 copy_multiply_fusion
  18.7 1.2 fusion.91
  20.2 12.3 %all_gather.45 = f32[2,256,256]{1,0,2:T(2,128)S(1)} all-gather(f32[2,256,64]{1,0,2:T(2,128)S(1)} %pad_maximum_fusion), channel_id=1, replica_groups=mesh['row'=8,'col_0'=8,'col_1'=4] {'col_1'}, dimensions={2}, use_global_device_ids=true | all-gather | bytes 655360 | tf_op jit(solution)/shard_map/all_gather | solution.py:45
  32.4 1.0 copy.25
  33.5 0.7 broadcast_in_dim.16
  34.1 7.6 %all-to-all-start = ((f32[8,6,256,2]{2,3,1,0:T(2,128)}), f32[8,6,256,2]{2,3,1,0:T(2,128)S(1)}, u32[]{:S(2)}, u32[]{:S(2)}) async-start(f32[8,6,256,2]{2,3,1,0:T(2,128)} %broadcast_in_dim.16), calls=%async_computation | async-start | bytes 196608 | tf_op jit(solution)/shard_map/all_to_all | solution.py:22
  41.8 0.3 iota_compare_fusion
  42.1 10.7 %broadcast_select_fusion = f32[6,2048,256]{2,1,0:T(8,128)} fusion(f32[6,2048,256]{2,1,0:T(8,128)} %param.18, pred[2048,256]{1,0:T(8,128)(4,1)S(1)} %iota_compare_fusion), kind=kLoop, calls=%fused_computation | loop fusion | flops 3145728 | bytes 25690112 | tf_op jit(solution)/shard_map/jit(_where)/select_n | solution.py:83
  52.9 0.6 fusion.92
  53.5 2.9 fusion.53
  56.6 36.2 %all-gather.10.cloned.1.call-done = f32[2,256,2048]{2,1,0:T(8,128)} async-done(((f32[2,256,256]{2,1,0:T(8,128)}), f32[2,256,2048]{2,1,0:T(8,128)}) %all-gather.10.cloned.1.call-update) | async-done | bytes 4194320 | tf_op jit(solution)/shard_map/all_gather | solution.py:45
  92.8 5.8 convolution_bitcast_fusion.4
  104.0 11.7 %all_gather.48 = f32[2,256,256]{1,0,2:T(2,128)S(1)} all-gather(f32[2,256,64]{1,0,2:T(2,128)S(1)} %pad_maximum_fusion.1), channel_id=1, replica_groups=mesh['row'=8,'col_0'=8,'col_1'=4] {'col_1'}, dimensions={2}, use_global_device_ids=true | all-gather | bytes 655360 | tf_op jit(solution)/shard_map/all_gather | solution.py:45
  115.7 1.0 copy.26
  116.9 12.6 %reduce-scatter.6.cloned.1.call-done = f32[256,66]{0,1:T(8,128)} async-done(((f32[2048,66]{0,1:T(8,128)}), f32[256,66]{0,1:T(8,128)}) %reduce-scatter.6.cloned.1.call-update) | async-done | bytes 67600 | tf_op jit(solution)/shard_map/reduce_scatter | solution.py:37
  129.6 16.2 %all_gather.47 = f32[2048,66]{0,1:T(8,128)S(1)} all-gather(f32[256,66]{0,1:T(8,128)} %reduce-scatter.6.cloned.1.call-done), channel_id=1, replica_groups=mesh['row'=8,'col_0'=8,'col_1'=4] {'row'}, dimensions={0}, use_global_device_ids=true | all-gather | bytes 608256 | tf_op jit(solution)/shard_map/all_gather | solution.py:38
  145.9 2.9 fusion.52
  148.9 37.9 %all-gather.12.cloned.1.call-done = f32[2,256,2048]{2,1,0:T(8,128)} async-done(((f32[2,256,256]{2,1,0:T(8,128)}), f32[2,256,2048]{2,1,0:T(8,128)}) %all-gather.12.cloned.1.call-update) | async-done | bytes 4194320 | tf_op jit(solution)/shard_map/all_gather | solution.py:45
  186.8 5.7 convolution_bitcast_fusion.3
  192.6 31.5 %reduce-scatter.8.cloned.1.call-done = f32[256,130]{0,1:T(8,128)} async-done(((f32[2048,130]{0,1:T(8,128)}), f32[256,130]{0,1:T(8,128)}) %reduce-scatter.8.cloned.1.call-update) | async-done | bytes 133136 | tf_op jit(solution)/shard_map/reduce_scatter | solution.py:37
  224.2 10.0 %all_gather.51 = f32[2,256,256]{1,0,2:T(2,128)S(1)} all-gather(f32[2,256,64]{1,0,2:T(2,128)S(1)} %pad_maximum_fusion.2), channel_id=1, replica_groups=mesh['row'=8,'col_0'=8,'col_1'=4] {'col_1'}, dimensions={2}, use_global_device_ids=true | all-gather | bytes 655360 | tf_op jit(solution)/shard_map/all_gather | solution.py:45
  234.2 1.0 copy.27
  235.3 18.0 %all-gather.14.cloned.1.call-done = f32[2048,130]{0,1:T(8,128)} async-done(((f32[256,130]{0,1:T(8,128)}), f32[2048,130]{0,1:T(8,128)}) %all-gather.14.cloned.1.call-update) | async-done | bytes 1064976 | tf_op jit(solution)/shard_map/all_gather | solution.py:38
  253.3 0.8 slice_subtract_fusion.3
  254.1 1.3 slice_negate_fusion.3
  255.5 3.2 fusion.48
  258.8 50.4 %all-gather.16.cloned.1.call-done = f32[2,256,2048]{2,1,0:T(8,128)} async-done(((f32[2,256,256]{2,1,0:T(8,128)}), f32[2,256,2048]{2,1,0:T(8,128)}) %all-gather.16.cloned.1.call-update) | async-done | bytes 4194320 | tf_op jit(solution)/shard_map/all_gather | solution.py:45
  309.2 6.6 convolution_bitcast_fusion.2
  315.9 32.2 %reduce-scatter.10.cloned.1.call-done = f32[256,194]{0,1:T(8,128)} async-done(((f32[2048,194]{0,1:T(8,128)}), f32[256,194]{0,1:T(8,128)}) %reduce-scatter.10.cloned.1.call-update) | async-done | bytes 198672 | tf_op jit(solution)/shard_map/reduce_scatter | solution.py:37
  353.2 2.4 multiply_bitcast_fusion.1
  355.8 9.9 %all_gather.54 = f32[2,256,256]{1,0,2:T(2,128)S(1)} all-gather(f32[2,256,64]{1,0,2:T(2,128)S(1)} %pad_maximum_fusion.3), channel_id=1, replica_groups=mesh['row'=8,'col_0'=8,'col_1'=4] {'col_1'}, dimensions={2}, use_global_device_ids=true | all-gather | bytes 655360 | tf_op jit(solution)/shard_map/all_gather | solution.py:45
  365.7 1.1 copy.28
  367.1 11.5 %all-gather.18.cloned.1.call-done = f32[2048,194]{0,1:T(8,128)} async-done(((f32[256,194]{0,1:T(8,128)}), f32[2048,194]{0,1:T(8,128)}) %all-gather.18.cloned.1.call-update) | async-done | bytes 1589264 | tf_op jit(solution)/shard_map/all_gather | solution.py:38
  378.6 0.8 slice_subtract_fusion.2
  379.4 1.5 slice_negate_fusion.2
  380.9 3.6 fusion.42
  384.6 50.2 %all-gather.20.cloned.1.call-done = f32[2,256,2048]{2,1,0:T(8,128)} async-done(((f32[2,256,256]{2,1,0:T(8,128)}), f32[2,256,2048]{2,1,0:T(8,128)}) %all-gather.20.cloned.1.call-update) | async-done | bytes 4194320 | tf_op jit(solution)/shard_map/all_gather | solution.py:45
  434.8 7.5 %convolution_bitcast_fusion.1 = f32[2048,258]{0,1:T(8,128)} fusion(f32[2,256,2048]{2,1,0:T(8,128)} %all-gather.20.cloned.1.call-done, f32[1,256,258]{1,2,0:T(8,128)S(1)} %slice_bitcast_fusion.36, f32[1,256,258]{1,2,0:T(8,128)S(1)} %slice_bitcast_fusion.37), kind=kOutput, calls=%fused_computation.9 | convolution fusion | flops 3246523392 | bytes 6836224 | tf_op jit(solution)/shard_map/tiw,tin->wn/dot_general | solution.py:55
  442.3 33.0 %reduce-scatter.12.cloned.1.call-done = f32[256,258]{0,1:T(8,128)} async-done(((f32[2048,258]{0,1:T(8,128)}), f32[256,258]{0,1:T(8,128)}) %reduce-scatter.12.cloned.1.call-update) | async-done | bytes 264208 | tf_op jit(solution)/shard_map/reduce_scatter | solution.py:37
  475.6 9.9 %all_gather.57 = f32[2,256,256]{1,0,2:T(2,128)S(1)} all-gather(f32[2,256,64]{1,0,2:T(2,128)S(1)} %pad_maximum_fusion.4), channel_id=1, replica_groups=mesh['row'=8,'col_0'=8,'col_1'=4] {'col_1'}, dimensions={2}, use_global_device_ids=true | all-gather | bytes 655360 | tf_op jit(solution)/shard_map/all_gather | solution.py:45
  485.5 1.0 copy.29
  486.8 20.1 %all-gather.22.cloned.1.call-done = f32[2048,258]{0,1:T(8,128)} async-done(((f32[256,258]{0,1:T(8,128)}), f32[2048,258]{0,1:T(8,128)}) %all-gather.22.cloned.1.call-update) | async-done | bytes 2113552 | tf_op jit(solution)/shard_map/all_gather | solution.py:38
  506.9 0.8 slice_subtract_fusion.1
  507.8 1.7 slice_negate_fusion.1
  509.5 4.0 fusion.36
  513.6 0.7 slice_bitcast_fusion.35
  514.3 48.8 %all-gather.24.cloned.1.call-done = f32[2,256,2048]{2,1,0:T(8,128)} async-done(((f32[2,256,256]{2,1,0:T(8,128)}), f32[2,256,2048]{2,1,0:T(8,128)}) %all-gather.24.cloned.1.call-update) | async-done | bytes 4194320 | tf_op jit(solution)/shard_map/all_gather | solution.py:45
  563.2 8.4 %convolution_bitcast_fusion = f32[2048,322]{0,1:T(8,128)} fusion(f32[2,256,2048]{2,1,0:T(8,128)} %all-gather.24.cloned.1.call-done, f32[1,256,322]{1,2,0:T(8,128)S(1)} %slice_bitcast_fusion.34, f32[1,256,322]{1,2,0:T(8,128)} %slice_bitcast_fusion.35), kind=kOutput, calls=%fused_computation.8 | convolution fusion | flops 4051862528 | bytes 7491584 | tf_op jit(solution)/shard_map/tiw,tin->wn/dot_general | solution.py:55
  571.6 34.0 %reduce-scatter.14.cloned.1.call-done = f32[256,322]{0,1:T(8,128)} async-done(((f32[2048,322]{0,1:T(8,128)}), f32[256,322]{0,1:T(8,128)}) %reduce-scatter.14.cloned.1.call-update) | async-done | bytes 329744 | tf_op jit(solution)/shard_map/reduce_scatter | solution.py:37
  605.6 32.0 %all-gather.26.cloned.1.call-done = f32[2048,322]{0,1:T(8,128)} async-done(((f32[256,322]{0,1:T(8,128)}), f32[2048,322]{0,1:T(8,128)}) %all-gather.26.cloned.1.call-update) | async-done | bytes 2637840 | tf_op jit(solution)/shard_map/all_gather | solution.py:38
  637.6 1.9 slice_negate_fusion
  639.6 0.8 slice_subtract_fusion
  640.4 4.4 fusion.30
  645.0 0.7 broadcast_in_dim.18
  645.7 9.5 %all-to-all-start.1 = ((f32[32,6,256]{2,1,0:T(8,128)}), f32[32,6,256]{2,1,0:T(8,128)S(1)}, u32[]{:S(2)}, u32[]{:S(2)}) async-start(f32[32,6,256]{2,1,0:T(8,128)} %broadcast_in_dim.18), calls=%async_computation.6 | async-start | bytes 524288 | tf_op jit(solution)/shard_map/all_to_all | solution.py:22
  655.2 0.6 slice.388
  655.8 11.1 %all-to-all-done.1 = f32[32,6,256]{2,1,0:T(8,128)S(1)} async-done(((f32[32,6,256]{2,1,0:T(8,128)}), f32[32,6,256]{2,1,0:T(8,128)S(1)}, u32[]{:S(2)}, u32[]{:S(2)}) %all-to-all-start.1) | async-done | bytes 196640 | tf_op jit(solution)/shard_map/all_to_all | solution.py:22
  666.9 0.6 reduce_sum.59
  (69 shorter events, 4.1 us)
Async XLA Ops:
  7.2 85.7 %all-gather.10.cloned.1.call-start = ((), (), s32[]{:S(2)}) async-start(), calls=%async_computation.7 | async-start | bytes 4718592 | tf_op jit(solution)/shard_map/all_gather | solution.py:45
  19.9 13.6 %copy-start.2 = (f32[6,256,2]{1,2,0:T(2,128)S(1)}, f32[6,256,2]{1,2,0:T(2,128)}, u32[]{:S(2)}) copy-start(f32[6,256,2]{1,2,0:T(2,128)} %param.21) | copy-start | bytes 36868
  34.1 18.8 %all-to-all-start = ((f32[8,6,256,2]{2,3,1,0:T(2,128)}), f32[8,6,256,2]{2,3,1,0:T(2,128)S(1)}, u32[]{:S(2)}, u32[]{:S(2)}) async-start(f32[8,6,256,2]{2,3,1,0:T(2,128)} %broadcast_in_dim.16), calls=%async_computation | async-start | bytes 196608 | tf_op jit(solution)/shard_map/all_to_all | solution.py:22
  41.8 87.8 %reduce-scatter.6.cloned.1.call-start = ((), (), s32[]{:S(2)}) async-start(), calls=%async_computation.8 | async-start | bytes 663552 | tf_op jit(solution)/shard_map/reduce_scatter | solution.py:37
  98.6 88.2 %all-gather.12.cloned.1.call-start = ((), (), s32[]{:S(2)}) async-start(), calls=%async_computation.9 | async-start | bytes 4718592 | tf_op jit(solution)/shard_map/all_gather | solution.py:45
  116.7 107.3 %reduce-scatter.8.cloned.1.call-start = ((), (), s32[]{:S(2)}) async-start(), calls=%async_computation.10 | async-start | bytes 1253376 | tf_op jit(solution)/shard_map/reduce_scatter | solution.py:37
  192.5 60.8 %all-gather.14.cloned.1.call-start = ((), (), s32[]{:S(2)}) async-start(), calls=%async_computation.11 | async-start | bytes 1253376 | tf_op jit(solution)/shard_map/all_gather | solution.py:38
  224.1 85.2 %all-gather.16.cloned.1.call-start = ((), (), s32[]{:S(2)}) async-start(), calls=%async_computation.12 | async-start | bytes 4718592 | tf_op jit(solution)/shard_map/all_gather | solution.py:45
  235.3 112.9 %reduce-scatter.10.cloned.1.call-start = ((), (), s32[]{:S(2)}) async-start(), calls=%async_computation.13 | async-start | bytes 1843200 | tf_op jit(solution)/shard_map/reduce_scatter | solution.py:37
  315.9 62.7 %all-gather.18.cloned.1.call-start = ((), (), s32[]{:S(2)}) async-start(), calls=%async_computation.14 | async-start | bytes 1843200 | tf_op jit(solution)/shard_map/all_gather | solution.py:38
  348.1 86.7 %all-gather.20.cloned.1.call-start = ((), (), s32[]{:S(2)}) async-start(), calls=%async_computation.15 | async-start | bytes 4718592 | tf_op jit(solution)/shard_map/all_gather | solution.py:45
  366.8 108.6 %reduce-scatter.12.cloned.1.call-start = ((), (), s32[]{:S(2)}) async-start(), calls=%async_computation.16 | async-start | bytes 2433024 | tf_op jit(solution)/shard_map/reduce_scatter | solution.py:37
  442.3 33.2 %copy-start = (f32[1,256,64]{1,0,2:T(1,128)S(1)}, f32[1,256,64]{1,0,2:T(1,128)}, u32[]{:S(2)}) copy-start(f32[1,256,64]{1,0,2:T(1,128)} %get-tuple-element.88) | copy-start | bytes 196612
  442.3 64.7 %copy-start.1 = (f32[1,8,256,2]{2,3,0,1:T(2,128)S(1)}, f32[1,8,256,2]{2,3,0,1:T(2,128)}, u32[]{:S(2)}) copy-start(f32[1,8,256,2]{2,3,0,1:T(2,128)} %get-tuple-element.98) | copy-start | bytes 49156
  442.3 64.6 %all-gather.22.cloned.1.call-start = ((), (), s32[]{:S(2)}) async-start(), calls=%async_computation.17 | async-start | bytes 2433024 | tf_op jit(solution)/shard_map/all_gather | solution.py:38
  475.4 87.8 %all-gather.24.cloned.1.call-start = ((), (), s32[]{:S(2)}) async-start(), calls=%async_computation.18 | async-start | bytes 4718592 | tf_op jit(solution)/shard_map/all_gather | solution.py:45
  486.5 119.1 %reduce-scatter.14.cloned.1.call-start = ((), (), s32[]{:S(2)}) async-start(), calls=%async_computation.19 | async-start | bytes 3022848 | tf_op jit(solution)/shard_map/reduce_scatter | solution.py:37
  571.6 66.1 %all-gather.26.cloned.1.call-start = ((), (), s32[]{:S(2)}) async-start(), calls=%async_computation.20 | async-start | bytes 3022848 | tf_op jit(solution)/shard_map/all_gather | solution.py:38
  645.7 21.2 %all-to-all-start.1 = ((f32[32,6,256]{2,1,0:T(8,128)}), f32[32,6,256]{2,1,0:T(8,128)S(1)}, u32[]{:S(2)}, u32[]{:S(2)}) async-start(f32[32,6,256]{2,1,0:T(8,128)} %broadcast_in_dim.18), calls=%async_computation.6 | async-start | bytes 524288 | tf_op jit(solution)/shard_map/all_to_all | solution.py:22
Sparse Core Ops, SparseCore 0:
  33.6 59.1 all-gather.9
  98.7 30.7 reduce-scatter.5
  131.4 55.4 all-gather.11
  192.6 31.3 reduce-scatter.7
  225.7 27.5 all-gather.13
  254.9 54.2 all-gather.15
  316.0 32.0 reduce-scatter.9
  350.0 28.5 all-gather.17
  380.4 54.3 all-gather.19
  442.4 32.9 reduce-scatter.11
  477.2 29.6 all-gather.21
  508.6 54.5 all-gather.23
  571.7 33.8 reduce-scatter.13
  607.3 30.3 all-gather.25
where the time goes:
time: 683 us; the launch traced here: 675 us
  waiting for transfers between devices  460 us (67%)
  blocking collectives  70 us (10%)
  matrix products  54.8 us (8%)
  other arithmetic  32 us (5%)
  between operations  27.1 us (4%)
  starting transfers between devices  18.2 us (3%)
  local copies, waits for them, and re-layouts  12.8 us (2%)
    all_gather x5, waiting for transfers between devices, gathered_by_axis(): nearer = lax.all_gather(array, axes[-1], axis=dim, tiled=True)  224 us
    reduce_scatter x5, waiting for transfers between devices, total_of(): own = lax.psum_scatter(padded, axis, scatter_dimension=0, tiled=True)  143 us
    all_gather x4, waiting for transfers between devices, total_of(): whole = lax.all_gather(own, axis, axis=0, tiled=True)  81.6 us
    all_gather x5, blocking collectives, gathered_by_axis(): nearer = lax.all_gather(array, axes[-1], axis=dim, tiled=True)  53.7 us
    dot_general x5, matrix products, contract(): return jnp.einsum('tiw,tin->wn', panel_piece, selected, precision=HIGHEST)  33.9 us
    dot_general x6, matrix products, body(): jnp.dot(lower_inv[current_sup].T, right, precision=HIGHEST, preferred_ele...  21 us
    all_to_all x2, starting transfers between devices, from_everyone(): return lax.all_to_all(copies, axis, split_axis=0, concat_axis=0, tiled=True)  17.2 us
    all_gather x1, blocking collectives, total_of(): whole = lax.all_gather(own, axis, axis=0, tiled=True)  16.2 us
  transfers between devices with their start and end apart: 16, of which 15 were waited for; matrix products, arithmetic and copies ran while one was open for 7% of the time, Pallas kernels for 0%

commit v1 on v0

v1 whole, which is shorter than its diff:
```python
import functools

import jax
import jax.numpy as jnp
from jax import lax
from jax.experimental import pallas as pl
from jax.experimental.pallas import tpu as pltpu
from jax.sharding import Mesh
from jax.sharding import PartitionSpec as P

NS = 6
MESH = pl.DeviceIdType.MESH
F32 = jnp.float32
BF16 = jnp.bfloat16
GROUPS = (
    ((4, 0), (3, 0)),
    ((2, 0), (1, 0)),
    ((2, 1), (3, 1)),
    ((0, 1), (1, 1)),
    ((0, 0), None),
)
PLACE = {4: (0, 0), 2: (0, 1), 0: (0, 2), 3: (1, 0), 1: (1, 1), 5: (1, 2)}
NT = (((1,), (1,)), ((), ()))
NN = (((1,), (0,)), ((), ()))


def halves(value):
    high = value.astype(BF16)
    return high, (value - high.astype(F32)).astype(BF16)


def mm(left, right, dims=NN):
    return lax.dot_general(left, right, dims, preferred_element_type=F32)


def ancestor_of(parent, sup, second):
    first = parent[sup]
    if not second:
        return first
    return jnp.where(first < NS, parent[jnp.minimum(first, NS - 1)], NS)


def slot_of(step, side):
    if side == 0:
        sup = jnp.where(step == 0, 4, jnp.where(step <= 2, 2, 0))
    else:
        sup = jnp.where((step == 0) | (step == 2), 3, 1)
    return sup, (step == 2) | (step == 3)


def slot_target(parent, step, side):
    sup, second = slot_of(step, side)
    first = parent[sup]
    above = jnp.where(first < NS, parent[jnp.minimum(first, NS - 1)], NS)
    return sup, jnp.where(second, above, first)


def local_kernel(parent, marks, d_lo, d_hi, b_lo, b_hi, part, blocks):
    step = pl.program_id(0)
    row_at = lax.axis_index("y") * 2 + lax.axis_index("core")
    lane = lax.broadcasted_iota(jnp.int32, (64, 256), 1)
    nothing = jnp.zeros((64, 256), BF16)
    weights = []
    for side, b_ref in ((0, b_lo), (1, b_hi)):
        sup, target = slot_target(parent, step, side)
        valid = target < NS
        if side == 1:
            valid = valid & (step < 4)
        kept = jnp.minimum(target, NS - 1)
        first = jnp.where(valid, marks[sup, 0, kept], 0).astype(F32)
        second = jnp.where(valid, marks[sup, 1, kept], 0).astype(F32)
        block = b_ref[0, 0] * jnp.where(lane < 128, first, second)
        blocks[0, side] = block
        high, low = halves(block)
        if side == 0:
            weights.append(jnp.concatenate([high, nothing, low, nothing], axis=0))
            weights.append(jnp.concatenate([high, nothing, nothing, nothing], axis=0))
        else:
            weights.append(jnp.concatenate([nothing, high, nothing, low], axis=0))
            weights.append(jnp.concatenate([nothing, high, nothing, nothing], axis=0))
    row_of = lax.broadcasted_iota(jnp.int32, (256, 256), 0)
    col_of = lax.broadcasted_iota(jnp.int32, (256, 256), 1) + row_at * 256
    for piece in range(8):
        rows = pl.ds(piece * 256, 256)
        keep = row_of + piece * 256 >= col_of
        lo_high, lo_low = halves(jnp.where(keep, d_lo[0, rows, :], 0.0))
        hi_high, hi_low = halves(jnp.where(keep, d_hi[0, rows, :], 0.0))
        total = mm(lo_high, weights[0], NT) + mm(lo_low, weights[1], NT)
        total = total + mm(hi_high, weights[2], NT) + mm(hi_low, weights[3], NT)
        part[piece // 2, piece % 2, 0] = total[:, :128] + total[:, 128:]


def local_products(parent, marks, diag_inv, blocks):
    def d_map(side):
        def at(step, parent, marks):
            _, target = slot_target(parent, step, side)
            return jnp.minimum(target, NS - 1), 0, 0

        return at

    def b_map(side):
        def at(step, parent, marks):
            sup, target = slot_target(parent, step, side)
            return jnp.minimum(target, NS - 1), sup, 0, 0

        return at

    return pl.pallas_call(
        local_kernel,
        out_shape=(
            jax.ShapeDtypeStruct((4, 2, 5, 256, 128), F32),
            jax.ShapeDtypeStruct((5, 2, 64, 256), F32),
        ),
        grid_spec=pltpu.PrefetchScalarGridSpec(
            num_scalar_prefetch=2,
            grid=(5,),
            in_specs=[
                pl.BlockSpec((1, 2048, 256), d_map(0)),
                pl.BlockSpec((1, 2048, 256), d_map(1)),
                pl.BlockSpec((1, 1, 64, 256), b_map(0)),
                pl.BlockSpec((1, 1, 64, 256), b_map(1)),
            ],
            out_specs=[
                pl.BlockSpec((4, 2, 1, 256, 128), lambda step, parent, marks: (0, 0, step, 0, 0)),
                pl.BlockSpec((1, 2, 64, 256), lambda step, parent, marks: (step, 0, 0, 0)),
            ],
        ),
        compiler_params=pltpu.CompilerParams(vmem_limit_bytes=60_000_000),
        cost_estimate=pl.CostEstimate(flops=4_000_000_000, bytes_accessed=30_000_000, transcendentals=0),
    )(parent, marks, diag_inv, diag_inv, blocks, blocks)


class Sems:
    def __init__(self, ref):
        self.ref, self.used = ref, 0

    def take(self):
        self.used += 1
        return self.ref.at[self.used - 1]


def sweep_kernel(
    parent, part, blocks, diag_inv, post, mean_out, var_out,
    part1, part2, core1, core2, first1, first2, second1, second2, home1, home2, all1, all2,
    spread, d_raw, d_high, d_low, post_all, post_high, post_low, l_high, l_low, x_high, x_low,
    solved, block_buf, sums, sums_x, sums_z, own_var, sends, recvs, locals_,
):
    y, k = lax.axis_index("y"), lax.axis_index("core")
    z, x = lax.axis_index("z"), lax.axis_index("x")
    r, c = y * 2 + k, z * 4 + x
    up, down, over = (y + 1) % 4, (y + 3) % 4, (y + 2) % 4
    send_sems, recv_sems = Sems(sends), Sems(recvs)
    pending = []

    def copy_to(src, dst, device):
        copy = pltpu.make_async_remote_copy(
            src_ref=src, dst_ref=dst, send_sem=send_sems.take(), recv_sem=recv_sems.take(),
            device_id=device, device_id_type=MESH,
        )
        copy.start()
        pending.append(copy)
        return copy

    def drain():
        while pending:
            pending.pop().wait_send()

    load1 = pltpu.make_async_copy(part.at[:, :, pl.ds(0, 2)], part1, locals_.at[0])
    load1.start()
    d_loads = []
    for order, sup in enumerate((4, 3, 2, 1, 0, 5)):
        load = pltpu.make_async_copy(diag_inv.at[sup], d_raw.at[sup], locals_.at[1 + order])
        load.start()
        d_loads.append((sup, load))
    load2 = pltpu.make_async_copy(part.at[:, :, pl.ds(2, 3)], part2, locals_.at[7])
    load2.start()
    load_b = pltpu.make_async_copy(blocks, block_buf, locals_.at[8])
    load_b.start()

    barrier = pltpu.get_barrier_semaphore()

    def greet(step, carry):
        there = (c + step) % 32
        pl.semaphore_signal(barrier, inc=1, device_id=(y, k, there // 4, there % 4), device_id_type=MESH)
        return carry

    lax.fori_loop(1, 32, greet, 0)
    for device in ((up, k, z, x), (down, k, z, x), (y, 1 - k, z, x)):
        pl.semaphore_signal(barrier, inc=1, device_id=device, device_id_type=MESH)
    pl.semaphore_wait(barrier, 34)

    def to_columns(source, target):
        send_sem, recv_sem = send_sems.take(), recv_sems.take()

        def one(step, carry):
            there = (c + step) % 32
            pltpu.make_async_remote_copy(
                src_ref=source(there), dst_ref=target(c), send_sem=send_sem, recv_sem=recv_sem,
                device_id=(y, k, there // 4, there % 4), device_id_type=MESH,
            ).start()
            return carry

        lax.fori_loop(1, 32, one, 0)
        return send_sem, recv_sem

    def bulk(sources, target, sems):
        return pltpu.make_async_remote_copy(
            src_ref=sources, dst_ref=target, send_sem=sems[0], recv_sem=sems[1],
            device_id=(y, k, z, (x + 1) % 4), device_id_type=MESH,
        )

    def reduce_rows(group_count, mine, core, first, second, home):
        swap = copy_to(mine.at[:, 1 - k], core, (y, 1 - k, z, x))
        yield
        swap.wait_recv()
        core[over] += mine[over, k]
        one_up = copy_to(core.at[over, :, pl.ds(0, 128)], first.at[0], (up, k, z, x))
        one_down = copy_to(core.at[over, :, pl.ds(128, 128)], first.at[1], (down, k, z, x))
        for there in (up, down, y):
            core[there] += mine[there, k]
        yield
        one_up.wait_recv()
        core[up, :, 0:128] += first[0]
        two_up = copy_to(core.at[up], second.at[0], (up, k, z, x))
        one_down.wait_recv()
        core[down, :, 128:256] += first[1]
        two_down = copy_to(core.at[down], second.at[1], (down, k, z, x))
        yield
        two_up.wait_recv()
        two_down.wait_recv()
        for group in range(group_count):
            value = core[y, group] + second[0, group] + second[1, group]
            home[:, group] = value.reshape(32, 8, 128)

    def share_rows(everyone, home):
        sems = to_columns(lambda there: home.at[there], lambda here: everyone.at[r, here])
        everyone[r, c] = home[c]
        yield
        both = bulk(home.at[pl.ds(0, 31)], everyone.at[r, pl.ds(0, 31)], sems)
        both.wait_recv()
        pending.append(both)
        below, above, beyond = down * 2 + k, up * 2 + k, over * 2 + k
        to_up = copy_to(everyone.at[r], everyone.at[r], (up, k, z, x))
        to_down = copy_to(everyone.at[r], everyone.at[r], (down, k, z, x))
        across = [copy_to(everyone.at[r], everyone.at[r], (y, 1 - k, z, x))]
        yield
        lower, upper = pl.ds(0, 16), pl.ds(16, 16)
        to_up.wait_recv()
        on_up = copy_to(everyone.at[below, lower], everyone.at[below, lower], (up, k, z, x))
        across.append(copy_to(everyone.at[below], everyone.at[below], (y, 1 - k, z, x)))
        to_down.wait_recv()
        on_down = copy_to(everyone.at[above, upper], everyone.at[above, upper], (down, k, z, x))
        across.append(copy_to(everyone.at[above], everyone.at[above], (y, 1 - k, z, x)))
        yield
        on_up.wait_recv()
        on_down.wait_recv()
        across.append(copy_to(everyone.at[beyond], everyone.at[beyond], (y, 1 - k, z, x)))
        yield
        for copy in across:
            copy.wait_recv()

    def ring(size, me, device, chunk, part_of):
        ahead, behind = (me + 1) % size, (me + size - 1) % size
        forth = copy_to(chunk(me), chunk(me), device(ahead))
        back = copy_to(chunk(me), chunk(me), device(behind))
        yield
        for step in range(1, size // 2):
            last = step == size // 2 - 1
            got_low, got_high = (me + size - step) % size, (me + step) % size
            forth.wait_recv()
            low = part_of(got_low, 0) if last else chunk(got_low)
            forth = copy_to(low, low, device(ahead))
            back.wait_recv()
            high = part_of(got_high, 1) if last else chunk(got_high)
            back = copy_to(high, high, device(behind))
            yield
        forth.wait_recv()
        back.wait_recv()

    def chained(*generators):
        for generator in generators:
            yield from generator()

    def run_together(*generators):
        live = list(generators)
        while live:
            for generator in list(live):
                try:
                    next(generator)
                except StopIteration:
                    live.remove(generator)

    lane64 = lax.broadcasted_iota(jnp.int32, (64, 128), 1) < 64
    lane8 = lax.broadcasted_iota(jnp.int32, (8, 128), 1) < 64

    def gather_left(everyone, group):
        for pair in range(16):
            even = everyone[:, 2 * pair, group].reshape(64, 128)
            odd = everyone[:, 2 * pair + 1, group].reshape(64, 128)
            cols = pl.ds(pair * 128, 128)
            for side, value in (
                (0, jnp.where(lane64, even, pltpu.roll(odd, 64, 1))),
                (1, jnp.where(lane64, pltpu.roll(even, 64, 1), odd)),
            ):
                high, low = halves(value)
                l_high[side, 0:64, cols] = high
                l_low[side, 0:64, cols] = low

    def gather_sums(everyone, group):
        for pair in range(16):
            even = jnp.sum(everyone[:, 2 * pair, group], axis=0)
            odd = jnp.sum(everyone[:, 2 * pair + 1, group], axis=0)
            cols = pl.ds(pair * 128, 128)
            blank = jnp.zeros((8, 128), F32)
            for side, value in (
                (0, jnp.where(lane8, even, pltpu.roll(odd, 64, 1))),
                (1, jnp.where(lane8, pltpu.roll(even, 64, 1), odd)),
            ):
                high, low = halves(jnp.concatenate([value, blank], axis=0))
                x_high[side, :, cols] = high
                x_low[side, :, cols] = low

    def times_d(sup, side, with_sums):
        highs, lows = l_high[side], l_low[side]
        if with_sums:
            highs = jnp.concatenate([highs, x_high[side]], axis=0)
            lows = jnp.concatenate([lows, x_low[side]], axis=0)
        value = mm(highs, d_high[sup]) + mm(lows, d_high[sup]) + mm(highs, d_low[sup])
        top = value[0:64]
        own_var[sup, :] = own_var[sup, :] + jnp.sum(top * top, axis=0)
        return value

    def put_mean(sup, rows):
        place = PLACE[sup][1]
        mean_out[sup] = rows[2 * place : 2 * place + 2]

    load1.wait()
    own_var[...] = jnp.zeros_like(own_var)
    round1 = reduce_rows(2, part1, core1, first1, second1, home1)
    next(round1)
    post_all[c] = post[...]
    post_sems = to_columns(lambda there: post, lambda here: post_all.at[here])
    next(round1)

    row_of = lax.broadcasted_iota(jnp.int32, (256, 256), 0)
    col_of = lax.broadcasted_iota(jnp.int32, (256, 256), 1) + r * 256

    def split_d(sup, load):
        load.wait()

        def one(piece, total):
            rows = pl.ds(pl.multiple_of(piece * 256, 256), 256)
            value = jnp.where(row_of + piece * 256 >= col_of, d_raw[sup, rows, :], 0.0)
            high, low = halves(value)
            d_high[sup, rows, :] = high
            d_low[sup, rows, :] = low
            return total + jnp.sum(value * value, axis=0, keepdims=True)

        total = lax.fori_loop(0, 8, one, jnp.zeros((1, 256), F32))
        sums[sup, :] = total[0]

    split_d(*d_loads[0])
    split_d(*d_loads[1])
    next(round1)
    split_d(*d_loads[2])
    split_d(*d_loads[3])
    next(round1, None)
    share1 = share_rows(all1, home1)
    next(share1)
    split_d(*d_loads[4])
    split_d(*d_loads[5])
    next(share1)

    post_both = bulk(post_all.at[pl.ds(0, 31)], post_all.at[pl.ds(0, 31)], post_sems)
    post_both.wait_recv()
    pending.append(post_both)
    for sup in range(NS):
        rows = post_all[:, 2 * sup : 2 * sup + 2, :]
        value = jnp.concatenate([rows] * 4, axis=1).reshape(256, 256)
        high, low = halves(value)
        post_high[sup] = high
        post_low[sup] = low
    next(share1)
    pair_of = (lax.broadcasted_iota(jnp.int32, (256, 128), 0) % 8) // 2
    low_lanes = lax.broadcasted_iota(jnp.int32, (256, 128), 1) < 64

    def placed(sup, value):
        side, pair = PLACE[sup]
        here = low_lanes if side == 0 else jnp.logical_not(low_lanes)
        return jnp.where(here & (pair_of == pair), value, 0.0)

    pick_row = lax.broadcasted_iota(jnp.int32, (256, 128), 0)
    pick_col = lax.broadcasted_iota(jnp.int32, (256, 128), 1) % 64 + x * 64
    picker = jnp.where((pick_row == pick_col) & (r == c // 4), 1.0, 0.0).astype(BF16)
    right_sum = jnp.zeros((256, 128), F32)
    for sup in range(NS):
        value = mm(post_high[sup], picker) + mm(post_low[sup], picker)
        right_sum = right_sum + placed(sup, value)

    def minus_post(right_sum, home, group, slots):
        high, low = halves(home[:, group].reshape(256, 128))
        for slot in slots:
            if slot is None:
                continue
            sup, second = slot
            at = jnp.minimum(ancestor_of(parent, sup, second), NS - 1)
            value = mm(post_high[at], high) + mm(post_low[at], high) + mm(post_high[at], low)
            right_sum = right_sum - placed(sup, value)
        return right_sum

    next(share1)
    for group in range(2):
        right_sum = minus_post(right_sum, home1, group, GROUPS[group])
    next(share1, None)
    drain()

    for group in range(2):
        gather_left(all1, group)
        for side in range(2):
            sup = GROUPS[group][side][0]
            solved[sup] = times_d(sup, side, False)

    inner = []
    for sup in (4, 3, 2, 1):
        has_child = functools.reduce(jnp.logical_or, [parent[below] == sup for below in range(sup)])
        inner.append((sup, jnp.logical_and(parent[sup] < NS, has_child).astype(jnp.int32)))
    picks = []
    before = jnp.int32(0)
    for sup, is_inner in inner:
        picks.append((sup, [is_inner * (before == place).astype(jnp.int32) for place in range(2)]))
        before = before + is_inner
    for place in range(2):
        value = jnp.zeros((64, 256), F32)
        for sup, chosen in picks:
            value = value + solved[sup] * chosen[place].astype(F32)
        spread[z, x, place] = value.reshape(8, 8, 256)

    lower, upper = pl.ds(0, 4), pl.ds(4, 4)
    on_z = lambda there: (y, k, there, x)
    on_x = lambda there: (y, k, z, there)
    order_a = chained(
        lambda: ring(8, z, on_z, lambda i: spread.at[i, x, :, lower], lambda i, q: spread.at[i, x, q, lower]),
        lambda: ring(4, x, on_x, lambda i: spread.at[:, i, :, lower], lambda i, q: spread.at[:, i, q, lower]),
    )
    order_b = chained(
        lambda: ring(4, x, on_x, lambda i: spread.at[z, i, :, upper], lambda i, q: spread.at[z, i, q, upper]),
        lambda: ring(8, z, on_z, lambda i: spread.at[i, :, :, upper], lambda i, q: spread.at[i, :, q, upper]),
    )
    run_together(order_a, order_b)
    drain()

    load_b.wait()
    load2.wait()
    sources = ((2, (1, 0)), (3, (0, 1)), (0, (4, 0)), (1, (1, 1)))
    weights = []
    for place in range(2):
        pieces = []
        for sup, (group, side) in sources:
            chosen = jnp.int32(0)
            for inner_sup, flags in picks:
                if inner_sup > sup:
                    chosen = chosen + flags[place] * (parent[sup] == inner_sup).astype(jnp.int32)
            pieces.append(block_buf[group, side] * chosen.astype(F32))
        weights.append(halves(jnp.concatenate(pieces, axis=0)))
    for row_block in range(8):
        total = jnp.zeros((256, 256), F32)
        for place in range(2):
            high, low = halves(spread[:, :, place, row_block].reshape(256, 256))
            w_high, w_low = weights[place]
            total = total + mm(high, w_high, NT) + mm(low, w_high, NT) + mm(high, w_low, NT)
        at = (row_block // 2, row_block % 2)
        part2[at[0], at[1], 0] = part2[at[0], at[1], 0] - total[:, :128]
        part2[at[0], at[1], 1] = part2[at[0], at[1], 1] - total[:, 128:]

    for _ in reduce_rows(3, part2, core2, first2, second2, home2):
        pass
    for group in range(3):
        right_sum = minus_post(right_sum, home2, group, GROUPS[group + 2])
    home2[:, 3] = right_sum.reshape(32, 8, 128)
    for _ in share_rows(all2, home2):
        pass
    drain()

    gather_sums(all2, 3)
    for group in range(3):
        gather_left(all2, group)
        for side in range(2):
            slot = GROUPS[group + 2][side]
            if slot is None:
                continue
            value = times_d(slot[0], side, group < 2)
            if group < 2:
                put_mean(slot[0], value[64:80])
    for sup in (4, 5):
        side = PLACE[sup][0]
        highs, lows = x_high[side], x_low[side]
        put_mean(sup, mm(highs, d_high[sup]) + mm(lows, d_high[sup]) + mm(highs, d_low[sup]))

    copies = []
    for step in range(1, 4):
        copies.append(copy_to(own_var, sums_x.at[step - 1], (y, k, z, (x + step) % 4)))
    for copy in copies:
        copy.wait_recv()
    sums_z[0] = own_var[...] + sums_x[0] + sums_x[1] + sums_x[2]
    copies = []
    for step in range(1, 8):
        copies.append(copy_to(sums_z.at[0], sums_z.at[step], (y, k, (z + step) % 8, x)))
    for copy in copies:
        copy.wait_recv()
    total = sums[...]
    for step in range(8):
        total = total + sums_z[step]
    var_out[...] = total[0:NS]
    drain()


def sweep(parent, part, blocks, diag_inv, post):
    any_ = pl.BlockSpec(memory_space=pl.ANY)
    vmem = pl.BlockSpec(memory_space=pltpu.VMEM)
    smem = pl.BlockSpec(memory_space=pltpu.SMEM)
    return pl.pallas_call(
        sweep_kernel,
        out_shape=(jax.ShapeDtypeStruct((NS, 2, 256), F32), jax.ShapeDtypeStruct((NS, 256), F32)),
        in_specs=[smem, any_, any_, any_, vmem],
        out_specs=(vmem, vmem),
        scratch_shapes=[
            pltpu.VMEM((4, 2, 2, 256, 128), F32),
            pltpu.VMEM((4, 2, 3, 256, 128), F32),
            pltpu.VMEM((4, 2, 256, 128), F32),
            pltpu.VMEM((4, 3, 256, 128), F32),
            pltpu.VMEM((2, 2, 128, 128), F32),
            pltpu.VMEM((2, 3, 128, 128), F32),
            pltpu.VMEM((2, 2, 256, 128), F32),
            pltpu.VMEM((2, 3, 256, 128), F32),
            pltpu.VMEM((32, 2, 8, 128), F32),
            pltpu.VMEM((32, 4, 8, 128), F32),
            pltpu.VMEM((8, 32, 2, 8, 128), F32),
            pltpu.VMEM((8, 32, 4, 8, 128), F32),
            pltpu.VMEM((8, 4, 2, 8, 8, 256), F32),
            pltpu.VMEM((NS, 2048, 256), F32),
            pltpu.VMEM((NS, 2048, 256), BF16),
            pltpu.VMEM((NS, 2048, 256), BF16),
            pltpu.VMEM((32, 16, 256), F32),
            pltpu.VMEM((NS, 256, 256), BF16),
            pltpu.VMEM((NS, 256, 256), BF16),
            pltpu.VMEM((2, 64, 2048), BF16),
            pltpu.VMEM((2, 64, 2048), BF16),
            pltpu.VMEM((2, 16, 2048), BF16),
            pltpu.VMEM((2, 16, 2048), BF16),
            pltpu.VMEM((5, 64, 256), F32),
            pltpu.VMEM((5, 2, 64, 256), F32),
            pltpu.VMEM((8, 256), F32),
            pltpu.VMEM((3, 8, 256), F32),
            pltpu.VMEM((8, 8, 256), F32),
            pltpu.VMEM((8, 256), F32),
            pltpu.SemaphoreType.DMA((96,)),
            pltpu.SemaphoreType.DMA((96,)),
            pltpu.SemaphoreType.DMA((9,)),
        ],
        compiler_params=pltpu.CompilerParams(
            collective_id=0, has_side_effects=True, vmem_limit_bytes=66_000_000
        ),
        cost_estimate=pl.CostEstimate(flops=8_000_000_000, bytes_accessed=30_000_000, transcendentals=0),
    )(parent, part, blocks, diag_inv, post)


def body(factor, diag_inv, structure, parent, post):
    marks = jnp.transpose(structure, (0, 2, 1))
    blocks = jnp.transpose(factor, (0, 2, 3, 1))
    post_rows = jnp.pad(jnp.transpose(post, (0, 2, 1)).reshape(12, 256), ((0, 4), (0, 0)))
    part, kept = local_products(parent, marks, diag_inv, blocks)
    mean, variance = sweep(parent, part, kept, diag_inv, post_rows)
    return jnp.transpose(mean, (0, 2, 1)), variance


def solution(mesh):
    finer = Mesh(mesh.devices.reshape(4, 2, 8, 4), ("y", "core", "z", "x"))
    row, col = ("y", "core"), ("z", "x")
    placed = (
        P(None, row, None, col),
        P(None, None, row),
        P(None, None, row),
        P(),
        P(None, row, col),
    )
    return jax.shard_map(
        body,
        mesh=finer,
        in_specs=placed,
        out_specs=(P(None, row, col), P(None, row)),
        check_vma=False,
    )
```

time: 683 us -> 177 us (0.26); the launches traced: 675 us -> 175 us
  waiting for transfers between devices: 460 us -> 0 us
  Pallas kernels: 0 us -> 171 us
  blocking collectives: 70 us -> 0 us
  matrix products: 54.8 us -> 0 us
  other arithmetic: 32 us -> 0 us
  between operations: 27.1 us -> 0.64 us
  starting transfers between devices: 18.2 us -> 0 us
  local copies, waits for them, and re-layouts: 12.8 us -> 3.93 us
    all_gather x9 -> x0, waiting for transfers between devices: 305 us -> none  [the longest x5 224 us: gathered_by_axis(): nearer = lax.all_gather(array, axes[-1], axis=dim, tiled=True)]
    pallas_call x0 -> x2, Pallas kernels: none -> 171 us  [the longest x1 159 us: sweep(): pl.pallas_call(sweep_kernel, out_shape=(jax.ShapeDtypeStruct((NS, 2, 256)...]
    reduce_scatter x5 -> x0, waiting for transfers between devices: 143 us -> none  [total_of(): own = lax.psum_scatter(padded, axis, scatter_dimension=0, tiled=True)]
    all_gather x6 -> x0, blocking collectives: 70 us -> none  [the longest x5 53.7 us: gathered_by_axis(): nearer = lax.all_gather(array, axes[-1], axis=dim, tiled=True)]
    dot_general x11 -> x0, matrix products: 54.8 us -> none  [the longest x5 33.9 us: contract(): return jnp.einsum('tiw,tin->wn', panel_piece, selected, precision=HIGHEST)]
    all_to_all x2 -> x0, starting transfers between devices: 17.2 us -> none  [from_everyone(): return lax.all_to_all(copies, axis, split_axis=0, concat_axis=0, tiled=True)]
    all_to_all x2 -> x0, waiting for transfers between devices: 11.1 us -> none  [from_everyone(): return lax.all_to_all(copies, axis, split_axis=0, concat_axis=0, tiled=True)]
    select_n x1 -> x0, other arithmetic: 10.7 us -> none  [body(): jnp.where((rows_full[:, None] >= own_cols[None, :])[None, :, :], diag_inv...]
  transfers between devices with their start and end apart: 16 -> 0, of which waited for: 15 -> 0; matrix products, arithmetic and copies ran while one was open for 7% -> 0% of each run, Pallas kernels for 0% -> 0%
where the time goes in v1:
time: 177 us; the launch traced here: 175 us
  Pallas kernels  171 us (97%)
  local copies, waits for them, and re-layouts  3.93 us (2%)
    pallas_call x1, Pallas kernels, sweep(): pl.pallas_call(sweep_kernel, out_shape=(jax.ShapeDtypeStruct((NS, 2, 256)...  159 us
    pallas_call x1, Pallas kernels, local_products(): pl.pallas_call(local_kernel, out_shape=(jax.ShapeDtypeStruct((4, 2, 5, 25...  12 us

profile of v1, /device:TPU:1, one launch (start us, length us, event | category | flops | bytes accessed | tf_op | source)
XLA Modules:
  0.0 175.5 jit_solution(16238194346765111909)
XLA Ops:
  0.6 0.7 reshape.7
  1.3 0.6 pad.4.post
  2.0 12.0 %shard_map.68 = (f32[4,2,5,256,128]{4,3,2,1,0:T(8,128)}, f32[5,2,64,256]{3,2,1,0:T(8,128)}) custom-call(s32[6]{0:T(128)} %parent.3, s32[6,2,6]{2,1,0:T(2,128)} %bitcast.8, f32[6,2048,256]{2,1,0:T(8,128)} %diag_inv.1, f32[6,2048,256]{2,1,0:T(8,128)} %diag_inv.1, f32[6,6,64,256]{3,2,1,0:T(8,128)} %bitcast.4, f32[6,6,64,256]{3,2,1,0:T(8,128)} %bitcast.5), custom_call_target="tpu_custom_call" | custom-call | flops 4000000000 | bytes 30000000 | tf_op jit(solution)/shard_map/pallas_call | solution.py:108
  13.9 158.9 %shard_map.69 = (f32[6,2,256]{2,1,0:T(2,128)}, f32[6,256]{1,0:T(8,128)}) custom-call(s32[6]{0:T(128)} %parent.3, f32[4,2,5,256,128]{4,3,2,1,0:T(8,128)} %get-tuple-element.6.part, f32[5,2,64,256]{3,2,1,0:T(8,128)} %get-tuple-element.7.blocks, f32[6,2048,256]{2,1,0:T(8,128)} %diag_inv.1, f32[16,256]{1,0:T(8,128)} %pad.4.post), custom_call_target="tpu_custom_call" | custom-call | flops 8000000000 | bytes 30000000 | tf_op jit(solution)/shard_map/pallas_call | solution.py:521
  172.9 1.3 copy.9
  174.2 1.3 copy.10

commit v2 on v0

v2 whole, which is shorter than its diff:
```python
import functools

import jax
import jax.numpy as jnp
from jax import lax
from jax.experimental import pallas as pl
from jax.experimental.pallas import tpu as pltpu
from jax.sharding import Mesh
from jax.sharding import PartitionSpec as P

NS = 6
MESH = pl.DeviceIdType.MESH
F32 = jnp.float32
BF16 = jnp.bfloat16
FIRST = (((4, 0), None), ((2, 0), (3, 0)), ((0, 0), (1, 0)))
SECOND = (((2, 1), (3, 1)), ((0, 1), (1, 1)))
PLACE = {4: (0, 0), 2: (0, 1), 0: (0, 2), 3: (1, 0), 1: (1, 1), 5: (1, 2)}
NT = (((1,), (1,)), ((), ()))
NN = (((1,), (0,)), ((), ()))


def halves(value):
    high = value.astype(BF16)
    return high, (value - high.astype(F32)).astype(BF16)


def mm(left, right, dims=NN):
    return lax.dot_general(left, right, dims, preferred_element_type=F32)


def mm3(left, right, dims=NN):
    return mm(left[0], right[0], dims) + mm(left[1], right[0], dims) + mm(left[0], right[1], dims)


def ancestor_of(parent, sup, second):
    first = parent[sup]
    if not second:
        return first
    return jnp.where(first < NS, parent[jnp.minimum(first, NS - 1)], NS)


def inner_flags(parent):
    flags = {}
    for sup in (4, 3, 2, 1):
        has_child = functools.reduce(jnp.logical_or, [parent[below] == sup for below in range(sup)])
        flags[sup] = jnp.logical_and(parent[sup] < NS, has_child).astype(jnp.int32)
    return flags


class Sems:
    def __init__(self, ref):
        self.ref, self.used = ref, 0

    def take(self):
        self.used += 1
        return self.ref.at[self.used - 1]


def sweep_kernel(
    width, parent, marks, blocks, diag_inv, post, mean_out, var_out,
    part1, part2, core1, core2, once1, once2, twice1, twice2, home1, home2, all1, all2, all_up,
    spread, d_raw, d_high, d_low, block_buf, post_all, post_high, post_low, l_high, l_low,
    x_high, x_low, h_high, h_low, own_var, sums, sums_x, sums_z, sends, recvs, locals_,
):
    y, k = lax.axis_index("y"), lax.axis_index("core")
    z, x = lax.axis_index("z"), lax.axis_index("x")
    r, c = y * 2 + k, z * 4 + x
    up, down, over = (y + 1) % 4, (y + 3) % 4, (y + 2) % 4
    send_sems, recv_sems = Sems(sends), Sems(recvs)
    pending = []

    def copy_to(src, dst, device):
        copy = pltpu.make_async_remote_copy(
            src_ref=src, dst_ref=dst, send_sem=send_sems.take(), recv_sem=recv_sems.take(),
            device_id=device, device_id_type=MESH,
        )
        copy.start()
        pending.append(copy)
        return copy

    load_b = pltpu.make_async_copy(blocks, block_buf, locals_.at[6])
    load_b.start()
    d_order = (5, 4, 3, 2, 1, 0)

    def load_d(order):
        load = pltpu.make_async_copy(diag_inv.at[d_order[order]], d_raw.at[order % 3], locals_.at[order])
        load.start()
        return load

    d_loads = [load_d(order) for order in range(3)]

    barrier = pltpu.get_barrier_semaphore()

    def greet(step, carry):
        there = (c + step) % 32
        pl.semaphore_signal(barrier, inc=1, device_id=(y, k, there // 4, there % 4), device_id_type=MESH)
        return carry

    lax.fori_loop(1, 32, greet, 0)
    for device in ((up, k, z, x), (down, k, z, x), (y, 1 - k, z, x)):
        pl.semaphore_signal(barrier, inc=1, device_id=device, device_id_type=MESH)

    def to_columns(source, target):
        send_sem, recv_sem = send_sems.take(), recv_sems.take()

        def one(step, carry):
            there = (c + step) % 32
            pltpu.make_async_remote_copy(
                src_ref=source(there), dst_ref=target(c), send_sem=send_sem, recv_sem=recv_sem,
                device_id=(y, k, there // 4, there % 4), device_id_type=MESH,
            ).start()
            return carry

        lax.fori_loop(1, 32, one, 0)
        return send_sem, recv_sem

    def bulk(sources, target, sems):
        return pltpu.make_async_remote_copy(
            src_ref=sources, dst_ref=target, send_sem=sems[0], recv_sem=sems[1],
            device_id=(y, k, z, (x + 1) % 4), device_id_type=MESH,
        )

    def reduce_rows(part, core, once, twice, home, group):
        swaps = {}
        for name, there in (("over", over), ("up", up), ("down", down), ("own", y)):
            swaps[name] = copy_to(part.at[group, there, 1 - k], core.at[group, there], (y, 1 - k, z, x))
        yield
        swaps["over"].wait_recv()
        core[group, over] += part[group, over, k]
        one_up = copy_to(core.at[group, over, pl.ds(0, 128)], once.at[group, 0], (up, k, z, x))
        one_down = copy_to(core.at[group, over, pl.ds(128, 128)], once.at[group, 1], (down, k, z, x))
        for name, there in (("up", up), ("down", down), ("own", y)):
            swaps[name].wait_recv()
            core[group, there] += part[group, there, k]
        yield
        one_up.wait_recv()
        core[group, up, 0:128] += once[group, 0]
        two_up = copy_to(core.at[group, up], twice.at[group, 0], (up, k, z, x))
        one_down.wait_recv()
        core[group, down, 128:256] += once[group, 1]
        two_down = copy_to(core.at[group, down], twice.at[group, 1], (down, k, z, x))
        yield
        two_up.wait_recv()
        two_down.wait_recv()
        value = core[group, y] + twice[group, 0] + twice[group, 1]
        home[:, group] = value.reshape(32, 8, 128)

    def over_rows(everyone):
        below, above, beyond = down * 2 + k, up * 2 + k, over * 2 + k
        to_up = copy_to(everyone.at[r], everyone.at[r], (up, k, z, x))
        to_down = copy_to(everyone.at[r], everyone.at[r], (down, k, z, x))
        across = [copy_to(everyone.at[r], everyone.at[r], (y, 1 - k, z, x))]
        yield
        lower, upper = pl.ds(0, 16), pl.ds(16, 16)
        to_up.wait_recv()
        on_up = copy_to(everyone.at[below, lower], everyone.at[below, lower], (up, k, z, x))
        across.append(copy_to(everyone.at[below], everyone.at[below], (y, 1 - k, z, x)))
        to_down.wait_recv()
        on_down = copy_to(everyone.at[above, upper], everyone.at[above, upper], (down, k, z, x))
        across.append(copy_to(everyone.at[above], everyone.at[above], (y, 1 - k, z, x)))
        yield
        on_up.wait_recv()
        on_down.wait_recv()
        across.append(copy_to(everyone.at[beyond], everyone.at[beyond], (y, 1 - k, z, x)))
        yield
        for copy in across:
            copy.wait_recv()

    def share_rows(everyone, home):
        sems = to_columns(lambda there: home.at[there], lambda here: everyone.at[r, here])
        everyone[r, c] = home[c]
        yield
        both = bulk(home.at[pl.ds(0, 31)], everyone.at[r, pl.ds(0, 31)], sems)
        both.wait_recv()
        pending.append(both)
        yield from over_rows(everyone)

    def ring(size, me, device, chunk):
        ahead, behind = (me + 1) % size, (me + size - 1) % size
        forth = [copy_to(chunk(me, q), chunk(me, q), device(ahead)) for q in range(2)]
        back = [copy_to(chunk(me, q), chunk(me, q), device(behind)) for q in (1, 0)][::-1]
        yield
        for step in range(1, size // 2):
            last = step == size // 2 - 1
            got_low, got_high = (me + size - step) % size, (me + step) % size
            for q in range(2):
                forth[q].wait_recv()
                if not last or q == 0:
                    low = chunk(got_low, q)
                    forth[q] = copy_to(low, low, device(ahead))
                back[1 - q].wait_recv()
                if not last or q == 0:
                    high = chunk(got_high, 1 - q)
                    back[1 - q] = copy_to(high, high, device(behind))
            yield
        forth[0].wait_recv()
        back[1].wait_recv()

    def chained(*generators):
        for generator in generators:
            yield from generator()

    def run_together(*generators):
        live = list(generators)
        while live:
            for generator in list(live):
                try:
                    next(generator)
                except StopIteration:
                    live.remove(generator)

    row_of = lax.broadcasted_iota(jnp.int32, (256, 256), 0)
    col_of = lax.broadcasted_iota(jnp.int32, (256, 256), 1) + r * 256

    def split_d(order):
        sup = d_order[order]
        d_loads[order].wait()

        def one(piece, total):
            rows = pl.ds(pl.multiple_of(piece * 256, 256), 256)
            value = jnp.where(row_of + piece * 256 >= col_of, d_raw[order % 3, rows, :], 0.0)
            high, low = halves(value)
            d_high[sup, rows, :] = high
            d_low[sup, rows, :] = low
            return total + jnp.sum(value * value, axis=0, keepdims=True)

        total = lax.fori_loop(0, 8, one, jnp.zeros((1, 256), F32))
        sums[sup, :] = total[0]
        if order + 3 < NS:
            d_loads.append(load_d(order + 3))

    for order in range(5):
        split_d(order)
    load_b.wait()

    row_lane = lax.broadcasted_iota(jnp.int32, (64, 256), 1)

    def multiply(part, group, slots):
        nothing = jnp.zeros((64, 256), BF16)
        terms = []
        for side, slot in enumerate(slots):
            if slot is None:
                continue
            sup, second = slot
            target = ancestor_of(parent, sup, second)
            valid = target < NS
            at = jnp.minimum(target, NS - 1)
            upper_mark = jnp.where(valid, marks[sup, 0, at], 0).astype(F32)
            lower_mark = jnp.where(valid, marks[sup, 1, at], 0).astype(F32)
            block = block_buf[at, sup] * jnp.where(row_lane < 128, upper_mark, lower_mark)
            high, low = halves(block)
            if side == 0:
                both, one = [high, nothing, low, nothing], [high, nothing, nothing, nothing]
            else:
                both, one = [nothing, high, nothing, low], [nothing, high, nothing, nothing]
            terms.append((at, jnp.concatenate(both, axis=0), jnp.concatenate(one, axis=0)))
        for piece in range(8):
            rows = pl.ds(piece * 256, 256)
            total = jnp.zeros((256, 256), F32)
            for at, both, one in terms:
                total = total + mm(d_high[at, rows, :], both, NT) + mm(d_low[at, rows, :], one, NT)
            part[group, piece // 2, piece % 2] = total[:, :128] + total[:, 128:]

    sums1 = [reduce_rows(part1, core1, once1, twice1, home1, group) for group in range(3)]
    sums2 = [reduce_rows(part2, core2, once2, twice2, home2, group) for group in range(2)]
    own_var[...] = jnp.zeros_like(own_var)
    multiply(part1, 0, FIRST[0])
    pl.semaphore_wait(barrier, 34)
    next(sums1[0])
    post_all[c] = post[...]
    post_sems = to_columns(lambda there: post, lambda here: post_all.at[here])
    multiply(part1, 1, FIRST[1])
    next(sums1[1])
    next(sums1[0])
    multiply(part1, 2, FIRST[2])
    next(sums1[2])
    next(sums1[1])
    next(sums1[0])
    multiply(part2, 0, SECOND[0])
    next(sums1[2])
    next(sums1[1])
    multiply(part2, 1, SECOND[1])
    next(sums1[2])
    next(sums1[0], None)
    split_d(5)
    next(sums1[1], None)
    next(sums2[0])
    next(sums2[1])
    next(sums1[2], None)

    flags = inner_flags(parent)
    picks = []
    before = jnp.int32(0)
    for sup in (4, 3, 2, 1):
        picks.append((sup, [flags[sup] * (before == place).astype(jnp.int32) for place in range(width)]))
        before = before + flags[sup]
    where_of = {4: (0, 0), 2: (1, 0), 3: (1, 1), 1: (2, 1)}
    low_lanes = lax.broadcasted_iota(jnp.int32, (256, 128), 1) < 64
    firsts = [home1[:, tile].reshape(256, 128) for tile in range(3)]
    chosen = []
    for place in range(width):
        sides = [jnp.zeros((256, 128), F32), jnp.zeros((256, 128), F32)]
        for sup, weight in picks:
            tile, side = where_of[sup]
            sides[side] = sides[side] + firsts[tile] * weight[place].astype(F32)
        chosen.append(sides)
    rolled = lambda value: pltpu.roll(value, 64, 1)
    if width == 1:
        lo, hi = chosen[0]
        in_low = jnp.where(low_lanes, lo + rolled(hi), 0.0)
        spread[z, x] = jnp.where(low_lanes[0:128], in_low[0:128], rolled(in_low[128:256]))
    else:
        lo = chosen[0][0] + rolled(chosen[0][1])
        hi = rolled(chosen[1][0]) + chosen[1][1]
        spread[z, x] = jnp.where(low_lanes, lo, hi)

    size = width * 128
    quarter = size // 4
    on_z = lambda there: (y, k, there, x)
    on_x = lambda there: (y, k, z, there)
    quarter_of = lambda part_at: pl.ds(part_at * quarter, quarter)
    order_a = chained(
        lambda: ring(8, z, on_z, lambda i, q: spread.at[i, x, quarter_of(q)]),
        lambda: ring(4, x, on_x, lambda i, q: spread.at[:, i, quarter_of(q)]),
    )
    order_b = chained(
        lambda: ring(4, x, on_x, lambda i, q: spread.at[z, i, quarter_of(2 + q)]),
        lambda: ring(8, z, on_z, lambda i, q: spread.at[i, :, quarter_of(2 + q)]),
    )

    def up_copies():
        all_up[r] = home1[:, 1:3]
        yield from over_rows(all_up)

    pair_of = (lax.broadcasted_iota(jnp.int32, (256, 128), 0) % 8) // 2

    def placed(sup, value):
        side, pair = PLACE[sup]
        here = low_lanes if side == 0 else jnp.logical_not(low_lanes)
        return jnp.where(here & (pair_of == pair), value, 0.0)

    right_sum = [jnp.zeros((256, 128), F32)]

    def minus_post(home, group, slots):
        parts = halves(home[:, group].reshape(256, 128))
        for slot in slots:
            if slot is None:
                continue
            sup, second = slot
            at = jnp.minimum(ancestor_of(parent, sup, second), NS - 1)
            value = mm3((post_high[at], post_low[at]), parts)
            right_sum[0] = right_sum[0] - placed(sup, value)

    def right_sides():
        yield
        post_both = bulk(post_all.at[pl.ds(0, 31)], post_all.at[pl.ds(0, 31)], post_sems)
        post_both.wait_recv()
        pending.append(post_both)
        for sup in range(NS):
            rows = post_all[:, 2 * sup : 2 * sup + 2, :]
            value = jnp.concatenate([rows] * 4, axis=1).reshape(256, 256)
            high, low = halves(value)
            post_high[sup] = high
            post_low[sup] = low
        yield
        pick_row = lax.broadcasted_iota(jnp.int32, (256, 128), 0)
        pick_col = lax.broadcasted_iota(jnp.int32, (256, 128), 1) % 64 + x * 64
        picker = jnp.where((pick_row == pick_col) & (r == c // 4), 1.0, 0.0).astype(BF16)
        for sup in range(NS):
            value = mm(post_high[sup], picker) + mm(post_low[sup], picker)
            right_sum[0] = right_sum[0] + placed(sup, value)
        yield
        for group in range(3):
            minus_post(home1, group, FIRST[group])

    share1 = share_rows(all1, home1)
    run_together(
        order_a,
        order_b,
        chained(lambda: up_copies(), lambda: sums2[0]),
        sums2[1],
        right_sides(),
    )

    next(share1)
    for pair in range(16):
        cols = pl.ds(pair * 128, 128)
        even = spread[pair // 2, 2 * (pair % 2)]
        odd = spread[pair // 2, 2 * (pair % 2) + 1]
        wide = low_lanes[0:size]
        for side, value in (
            (0, jnp.where(wide, even, rolled(odd))),
            (1, jnp.where(wide, rolled(even), odd)),
        ):
            high, low = halves(value)
            rows = pl.ds(side * size, size)
            h_high[rows, cols] = high
            h_low[rows, cols] = low
    lane_256 = lax.broadcasted_iota(jnp.int32, (1, 256), 1)
    through = jnp.zeros((256, 256), F32)
    for place in range(width):
        keep = jnp.zeros((1, 256), F32)
        for at, sup in enumerate((2, 3, 0, 1)):
            chosen_here = jnp.int32(0)
            for inner_sup, weight in picks:
                if inner_sup > sup:
                    chosen_here = chosen_here + weight[place] * (parent[sup] == inner_sup).astype(jnp.int32)
            keep = keep + jnp.where(lane_256 // 64 == at, chosen_here.astype(F32), 0.0)
        for row_block in range(8):
            right = jnp.concatenate(
                [all_up[row_block, :, tile].reshape(256, 128) for tile in range(2)], axis=1
            )
            cols = pl.ds(row_block * 256, 256)
            rows = pl.ds(place * 256, 256)
            through = through + mm3((h_high[rows, cols], h_low[rows, cols]), halves(right * keep))
    for group in range(2):
        value = home2[:, group].reshape(256, 128) - through[:, group * 128 : group * 128 + 128]
        home2[:, group] = value.reshape(32, 8, 128)
    for group in range(2):
        minus_post(home2, group, SECOND[group])
    home2[:, 2] = right_sum[0].reshape(32, 8, 128)

    lane64 = low_lanes[0:64]
    lane8 = low_lanes[0:8]

    def gather_left(everyone, group):
        for pair in range(16):
            even = everyone[:, 2 * pair, group].reshape(64, 128)
            odd = everyone[:, 2 * pair + 1, group].reshape(64, 128)
            cols = pl.ds(pair * 128, 128)
            for side, value in (
                (0, jnp.where(lane64, even, rolled(odd))),
                (1, jnp.where(lane64, rolled(even), odd)),
            ):
                high, low = halves(value)
                l_high[side, 0:64, cols] = high
                l_low[side, 0:64, cols] = low

    def gather_sums(everyone, group):
        for pair in range(16):
            even = jnp.sum(everyone[:, 2 * pair, group], axis=0)
            odd = jnp.sum(everyone[:, 2 * pair + 1, group], axis=0)
            cols = pl.ds(pair * 128, 128)
            blank = jnp.zeros((8, 128), F32)
            for side, value in (
                (0, jnp.where(lane8, even, rolled(odd))),
                (1, jnp.where(lane8, rolled(even), odd)),
            ):
                high, low = halves(jnp.concatenate([value, blank], axis=0))
                x_high[side, :, cols] = high
                x_low[side, :, cols] = low

    def times_d(sup, side, with_sums):
        highs, lows = l_high[side], l_low[side]
        if with_sums:
            highs = jnp.concatenate([highs, x_high[side]], axis=0)
            lows = jnp.concatenate([lows, x_low[side]], axis=0)
        value = mm3((highs, lows), (d_high[sup], d_low[sup]))
        top = value[0:64]
        own_var[sup, :] = own_var[sup, :] + jnp.sum(top * top, axis=0)
        return value

    def put_mean(sup, rows):
        place = PLACE[sup][1]
        mean_out[sup] = rows[2 * place : 2 * place + 2]

    def products(everyone, group, slots, with_sums):
        gather_left(everyone, group)
        for side, slot in enumerate(slots):
            if slot is None:
                continue
            value = times_d(slot[0], side, with_sums)
            if with_sums:
                put_mean(slot[0], value[64:80])

    share2 = share_rows(all2, home2)
    next(share2)
    next(share1)
    next(share1)
    next(share2)
    next(share1)
    next(share1, None)
    next(share2)
    for group in range(3):
        products(all1, group, FIRST[group], False)
    next(share2)
    next(share2, None)
    gather_sums(all2, 2)
    for group in range(2):
        products(all2, group, SECOND[group], True)
    for sup in (4, 5):
        side = PLACE[sup][0]
        put_mean(sup, mm3((x_high[side], x_low[side]), (d_high[sup], d_low[sup])))

    copies = []
    for step in range(1, 4):
        copies.append(copy_to(own_var, sums_x.at[step - 1], (y, k, z, (x + step) % 4)))
    for copy in copies:
        copy.wait_recv()
    sums_z[0] = own_var[...] + sums_x[0] + sums_x[1] + sums_x[2]
    copies = []
    for step in range(1, 8):
        copies.append(copy_to(sums_z.at[0], sums_z.at[step], (y, k, (z + step) % 8, x)))
    for copy in copies:
        copy.wait_recv()
    total = sums[...]
    for step in range(8):
        total = total + sums_z[step]
    var_out[...] = total[0:NS]
    while pending:
        pending.pop().wait_send()


def sweep(width, parent, marks, blocks, diag_inv, post):
    any_ = pl.BlockSpec(memory_space=pl.ANY)
    vmem = pl.BlockSpec(memory_space=pltpu.VMEM)
    smem = pl.BlockSpec(memory_space=pltpu.SMEM)
    return pl.pallas_call(
        functools.partial(sweep_kernel, width),
        out_shape=(jax.ShapeDtypeStruct((NS, 2, 256), F32), jax.ShapeDtypeStruct((NS, 256), F32)),
        in_specs=[smem, smem, any_, any_, vmem],
        out_specs=(vmem, vmem),
        scratch_shapes=[
            pltpu.VMEM((3, 4, 2, 256, 128), F32),
            pltpu.VMEM((2, 4, 2, 256, 128), F32),
            pltpu.VMEM((3, 4, 256, 128), F32),
            pltpu.VMEM((2, 4, 256, 128), F32),
            pltpu.VMEM((3, 2, 128, 128), F32),
            pltpu.VMEM((2, 2, 128, 128), F32),
            pltpu.VMEM((3, 2, 256, 128), F32),
            pltpu.VMEM((2, 2, 256, 128), F32),
            pltpu.VMEM((32, 3, 8, 128), F32),
            pltpu.VMEM((32, 3, 8, 128), F32),
            pltpu.VMEM((8, 32, 3, 8, 128), F32),
            pltpu.VMEM((8, 32, 3, 8, 128), F32),
            pltpu.VMEM((8, 32, 2, 8, 128), F32),
            pltpu.VMEM((8, 4, width * 128, 128), F32),
            pltpu.VMEM((3, 2048, 256), F32),
            pltpu.VMEM((NS, 2048, 256), BF16),
            pltpu.VMEM((NS, 2048, 256), BF16),
            pltpu.VMEM((NS, NS, 64, 256), F32),
            pltpu.VMEM((32, 16, 256), F32),
            pltpu.VMEM((NS, 256, 256), BF16),
            pltpu.VMEM((NS, 256, 256), BF16),
            pltpu.VMEM((2, 64, 2048), BF16),
            pltpu.VMEM((2, 64, 2048), BF16),
            pltpu.VMEM((2, 16, 2048), BF16),
            pltpu.VMEM((2, 16, 2048), BF16),
            pltpu.VMEM((width * 256, 2048), BF16),
            pltpu.VMEM((width * 256, 2048), BF16),
            pltpu.VMEM((8, 256), F32),
            pltpu.VMEM((8, 256), F32),
            pltpu.VMEM((3, 8, 256), F32),
            pltpu.VMEM((8, 8, 256), F32),
            pltpu.SemaphoreType.DMA((160,)),
            pltpu.SemaphoreType.DMA((160,)),
            pltpu.SemaphoreType.DMA((7,)),
        ],
        compiler_params=pltpu.CompilerParams(
            collective_id=width - 1, has_side_effects=True, vmem_limit_bytes=67_000_000
        ),
        cost_estimate=pl.CostEstimate(flops=12_000_000_000, bytes_accessed=30_000_000, transcendentals=0),
    )(parent, marks, blocks, diag_inv, post)


def body(factor, diag_inv, structure, parent, post):
    marks = jnp.transpose(structure, (0, 2, 1))
    blocks = jnp.transpose(factor, (0, 2, 3, 1))
    post_rows = jnp.pad(jnp.transpose(post, (0, 2, 1)).reshape(12, 256), ((0, 4), (0, 0)))
    mean, variance = sweep(2, parent, marks, blocks, diag_inv, post_rows)
    return jnp.transpose(mean, (0, 2, 1)), variance


def solution(mesh):
    finer = Mesh(mesh.devices.reshape(4, 2, 8, 4), ("y", "core", "z", "x"))
    row, col = ("y", "core"), ("z", "x")
    placed = (
        P(None, row, None, col),
        P(None, None, row),
        P(None, None, row),
        P(),
        P(None, row, col),
    )
    return jax.shard_map(
        body,
        mesh=finer,
        in_specs=placed,
        out_specs=(P(None, row, col), P(None, row)),
        check_vma=False,
    )
```

time: 683 us -> 126 us (0.18); the launches traced: 675 us -> 125 us
  waiting for transfers between devices: 460 us -> 0 us
  Pallas kernels: 0 us -> 120 us
  blocking collectives: 70 us -> 0 us
  matrix products: 54.8 us -> 0 us
  other arithmetic: 32 us -> 0 us
  between operations: 27.1 us -> 0.64 us
  starting transfers between devices: 18.2 us -> 0 us
  local copies, waits for them, and re-layouts: 12.8 us -> 3.93 us
    all_gather x9 -> x0, waiting for transfers between devices: 305 us -> none  [the longest x5 224 us: gathered_by_axis(): nearer = lax.all_gather(array, axes[-1], axis=dim, tiled=True)]
    reduce_scatter x5 -> x0, waiting for transfers between devices: 143 us -> none  [total_of(): own = lax.psum_scatter(padded, axis, scatter_dimension=0, tiled=True)]
    pallas_call x0 -> x1, Pallas kernels: none -> 120 us  [sweep(): pl.pallas_call(functools.partial(sweep_kernel, width), out_shape=(jax.Sha...]
    all_gather x6 -> x0, blocking collectives: 70 us -> none  [the longest x5 53.7 us: gathered_by_axis(): nearer = lax.all_gather(array, axes[-1], axis=dim, tiled=True)]
    dot_general x11 -> x0, matrix products: 54.8 us -> none  [the longest x5 33.9 us: contract(): return jnp.einsum('tiw,tin->wn', panel_piece, selected, precision=HIGHEST)]
    all_to_all x2 -> x0, starting transfers between devices: 17.2 us -> none  [from_everyone(): return lax.all_to_all(copies, axis, split_axis=0, concat_axis=0, tiled=True)]
    all_to_all x2 -> x0, waiting for transfers between devices: 11.1 us -> none  [from_everyone(): return lax.all_to_all(copies, axis, split_axis=0, concat_axis=0, tiled=True)]
    select_n x1 -> x0, other arithmetic: 10.7 us -> none  [body(): jnp.where((rows_full[:, None] >= own_cols[None, :])[None, :, :], diag_inv...]
  transfers between devices with their start and end apart: 16 -> 0, of which waited for: 15 -> 0; matrix products, arithmetic and copies ran while one was open for 7% -> 0% of each run, Pallas kernels for 0% -> 0%
where the time goes in v2:
time: 126 us; the launch traced here: 125 us
  Pallas kernels  120 us (95%)
  local copies, waits for them, and re-layouts  3.93 us (3%)
    pallas_call x1, Pallas kernels, sweep(): pl.pallas_call(functools.partial(sweep_kernel, width), out_shape=(jax.Sha...  120 us
    unnamed x2, local copies, waits for them, and re-layouts  2.6 us

profile of v2, /device:TPU:1, one launch (start us, length us, event | category | flops | bytes accessed | tf_op | source)
XLA Modules:
  0.0 124.8 jit_solution(377191600839534283)
XLA Ops:
  0.6 0.7 reshape.7
  1.3 0.6 pad.4.post
  2.0 120.2 %shard_map.68 = (f32[6,2,256]{2,1,0:T(2,128)}, f32[6,256]{1,0:T(8,128)}) custom-call(s32[6]{0:T(128)} %parent.1, s32[6,2,6]{2,1,0:T(2,128)} %bitcast.7, f32[6,6,64,256]{3,2,1,0:T(8,128)} %bitcast.6, f32[6,2048,256]{2,1,0:T(8,128)} %diag_inv.1, f32[16,256]{1,0:T(8,128)} %pad.4.post), custom_call_target="tpu_custom_call" | custom-call | flops 12000000000 | bytes 30000000 | tf_op jit(solution)/shard_map/pallas_call | solution.py:518
  122.2 1.3 %copy.9 = f32[6,256,2]{1,2,0:T(2,128)} copy(f32[6,256,2]{1,2,0:T(2,128)} %bitcast.5) | data formatting | bytes 24576
  123.5 1.3 %copy.10 = f32[6,256]{1,0:T(8,128)} copy(f32[6,256]{1,0:T(8,128)} %get-tuple-element.9) | data formatting | bytes 12288

commit v3 on v2

--- a/solution.py
+++ b/solution.py
@@ -60,7 +60,7 @@
     width, parent, marks, blocks, diag_inv, post, mean_out, var_out,
     part1, part2, core1, core2, once1, once2, twice1, twice2, home1, home2, all1, all2, all_up,
     spread, d_raw, d_high, d_low, block_buf, post_all, post_high, post_low, l_high, l_low,
-    x_high, x_low, h_high, h_low, own_var, sums, sums_x, sums_z, sends, recvs, locals_,
+    x_high, x_low, h_high, h_low, post_rows, own_var, sums, sums_x, sums_z, sends, recvs, locals_,
 ):
     y, k = lax.axis_index("y"), lax.axis_index("core")
     z, x = lax.axis_index("z"), lax.axis_index("x")
@@ -100,8 +100,8 @@
     for device in ((up, k, z, x), (down, k, z, x), (y, 1 - k, z, x)):
         pl.semaphore_signal(barrier, inc=1, device_id=device, device_id_type=MESH)
 
-    def to_columns(source, target):
-        send_sem, recv_sem = send_sems.take(), recv_sems.take()
+    def to_columns(source, target, sems=None, steps=(1, 32)):
+        send_sem, recv_sem = sems or (send_sems.take(), recv_sems.take())
 
         def one(step, carry):
             there = (c + step) % 32
@@ -111,7 +111,7 @@
             ).start()
             return carry
 
-        lax.fori_loop(1, 32, one, 0)
+        lax.fori_loop(*steps, one, 0)
         return send_sem, recv_sem
 
     def bulk(sources, target, sems):
@@ -166,10 +166,13 @@
         for copy in across:
             copy.wait_recv()
 
-    def share_rows(everyone, home):
-        sems = to_columns(lambda there: home.at[there], lambda here: everyone.at[r, here])
+    def share_rows(everyone, home, pieces=1):
         everyone[r, c] = home[c]
-        yield
+        sems = None
+        for piece in range(pieces):
+            steps = (1 + 31 * piece // pieces, 1 + 31 * (piece + 1) // pieces)
+            sems = to_columns(lambda there: home.at[there], lambda here: everyone.at[r, here], sems, steps)
+            yield
         both = bulk(home.at[pl.ds(0, 31)], everyone.at[r, pl.ds(0, 31)], sems)
         both.wait_recv()
         pending.append(both)
@@ -200,14 +203,13 @@
         for generator in generators:
             yield from generator()
 
-    def run_together(*generators):
+    def run_together(generators, beside):
         live = list(generators)
         while live:
             for generator in list(live):
-                try:
-                    next(generator)
-                except StopIteration:
+                if next(generator, "end") == "end":
                     live.remove(generator)
+            next(beside, None)
 
     row_of = lax.broadcasted_iota(jnp.int32, (256, 256), 0)
     col_of = lax.broadcasted_iota(jnp.int32, (256, 256), 1) + r * 256
@@ -229,8 +231,7 @@
         if order + 3 < NS:
             d_loads.append(load_d(order + 3))
 
-    for order in range(5):
-        split_d(order)
+    split_d(0)
     load_b.wait()
 
     row_lane = lax.broadcasted_iota(jnp.int32, (64, 256), 1)
@@ -265,27 +266,34 @@
     sums2 = [reduce_rows(part2, core2, once2, twice2, home2, group) for group in range(2)]
     own_var[...] = jnp.zeros_like(own_var)
     multiply(part1, 0, FIRST[0])
+    for sup in range(NS):
+        post_rows[2 * sup : 2 * sup + 2, :] = post[sup]
+    post_rows[2 * NS : 16, :] = jnp.zeros((16 - 2 * NS, 256), F32)
     pl.semaphore_wait(barrier, 34)
     next(sums1[0])
-    post_all[c] = post[...]
-    post_sems = to_columns(lambda there: post, lambda here: post_all.at[here])
+    post_all[c] = post_rows[...]
+    post_sems = to_columns(lambda there: post_rows, lambda here: post_all.at[here])
+    split_d(1)
+    next(sums1[0])
+    split_d(2)
     multiply(part1, 1, FIRST[1])
     next(sums1[1])
     next(sums1[0])
+    split_d(3)
+    next(sums1[1])
+    split_d(4)
     multiply(part1, 2, FIRST[2])
     next(sums1[2])
+    next(sums1[0], None)
     next(sums1[1])
-    next(sums1[0])
+    next(sums1[2])
     multiply(part2, 0, SECOND[0])
+    next(sums1[1], None)
     next(sums1[2])
-    next(sums1[1])
     multiply(part2, 1, SECOND[1])
-    next(sums1[2])
-    next(sums1[0], None)
-    split_d(5)
-    next(sums1[1], None)
     next(sums2[0])
     next(sums2[1])
+    split_d(5)
     next(sums1[2], None)
 
     flags = inner_flags(parent)
@@ -373,16 +381,9 @@
         for group in range(3):
             minus_post(home1, group, FIRST[group])
 
-    share1 = share_rows(all1, home1)
-    run_together(
-        order_a,
-        order_b,
-        chained(lambda: up_copies(), lambda: sums2[0]),
-        sums2[1],
-        right_sides(),
-    )
-
-    next(share1)
+    share1 = share_rows(all1, home1, 4)
+    run_together((order_a, order_b, sums2[0], sums2[1], up_copies(), right_sides()), share1)
+
     for pair in range(16):
         cols = pl.ds(pair * 128, 128)
         even = spread[pair // 2, 2 * (pair % 2)]
@@ -475,14 +476,13 @@
 
     share2 = share_rows(all2, home2)
     next(share2)
-    next(share1)
-    next(share1)
+    for _ in share1:
+        pass
+    products(all1, 0, FIRST[0], False)
     next(share2)
-    next(share1)
-    next(share1, None)
+    products(all1, 1, FIRST[1], False)
     next(share2)
-    for group in range(3):
-        products(all1, group, FIRST[group], False)
+    products(all1, 2, FIRST[2], False)
     next(share2)
     next(share2, None)
     gather_sums(all2, 2)
@@ -548,6 +548,7 @@
             pltpu.VMEM((2, 16, 2048), BF16),
             pltpu.VMEM((width * 256, 2048), BF16),
             pltpu.VMEM((width * 256, 2048), BF16),
+            pltpu.VMEM((16, 256), F32),
             pltpu.VMEM((8, 256), F32),
             pltpu.VMEM((8, 256), F32),
             pltpu.VMEM((3, 8, 256), F32),
@@ -566,8 +567,7 @@
 def body(factor, diag_inv, structure, parent, post):
     marks = jnp.transpose(structure, (0, 2, 1))
     blocks = jnp.transpose(factor, (0, 2, 3, 1))
-    post_rows = jnp.pad(jnp.transpose(post, (0, 2, 1)).reshape(12, 256), ((0, 4), (0, 0)))
-    mean, variance = sweep(2, parent, marks, blocks, diag_inv, post_rows)
+    mean, variance = sweep(2, parent, marks, blocks, diag_inv, jnp.transpose(post, (0, 2, 1)))
     return jnp.transpose(mean, (0, 2, 1)), variance
 
 

time: 126 us -> 130 us (1.032)
  Pallas kernels: 120 us -> 127 us
  local copies, waits for them, and re-layouts: 3.93 us -> 2.6 us
    pallas_call x1, Pallas kernels: 120 us -> 127 us  [sweep(): pl.pallas_call(functools.partial(sweep_kernel, width), out_shape=(jax.Sha...]
where the time goes in v3:
time: 130 us
  Pallas kernels  127 us (98%)
  local copies, waits for them, and re-layouts  2.6 us (2%)
    pallas_call x1, Pallas kernels, sweep(): pl.pallas_call(functools.partial(sweep_kernel, width), out_shape=(jax.Sha...  127 us
    unnamed x2, local copies, waits for them, and re-layouts  2.6 us

profile of v3, /device:TPU:1, one launch (start us, length us, event | category | flops | bytes accessed | tf_op | source)
XLA Modules:
  0.0 129.9 jit_solution(4733337016540895417)
XLA Ops:
  0.6 126.7 %shard_map.68 = (f32[6,2,256]{2,1,0:T(2,128)}, f32[6,256]{1,0:T(8,128)}) custom-call(s32[6]{0:T(128)} %parent.1, s32[6,2,6]{2,1,0:T(2,128)} %bitcast.7, f32[6,6,64,256]{3,2,1,0:T(8,128)} %bitcast.5, f32[6,2048,256]{2,1,0:T(8,128)} %diag_inv.1, f32[6,2,256]{2,1,0:T(2,128)} %bitcast.6), custom_call_target="tpu_custom_call" | custom-call | flops 12000000000 | bytes 30000000 | tf_op jit(solution)/shard_map/pallas_call | solution.py:518
  127.3 1.3 %copy.9 = f32[6,256,2]{1,2,0:T(2,128)} copy(f32[6,256,2]{1,2,0:T(2,128)} %bitcast.4) | data formatting | bytes 24576
  128.6 1.3 copy.10

commit v4 on v3

--- a/solution.py
+++ b/solution.py
@@ -57,11 +57,12 @@
 
 
 def sweep_kernel(
-    width, parent, marks, blocks, diag_inv, post, mean_out, var_out,
+    early, parent, marks, blocks, diag_inv, post, mean_out, var_out,
     part1, part2, core1, core2, once1, once2, twice1, twice2, home1, home2, all1, all2, all_up,
     spread, d_raw, d_high, d_low, block_buf, post_all, post_high, post_low, l_high, l_low,
     x_high, x_low, h_high, h_low, post_rows, own_var, sums, sums_x, sums_z, sends, recvs, locals_,
 ):
+    width = 1 if early else 2
     y, k = lax.axis_index("y"), lax.axis_index("core")
     z, x = lax.axis_index("z"), lax.axis_index("x")
     r, c = y * 2 + k, z * 4 + x
@@ -100,8 +101,8 @@
     for device in ((up, k, z, x), (down, k, z, x), (y, 1 - k, z, x)):
         pl.semaphore_signal(barrier, inc=1, device_id=device, device_id_type=MESH)
 
-    def to_columns(source, target, sems=None, steps=(1, 32)):
-        send_sem, recv_sem = sems or (send_sems.take(), recv_sems.take())
+    def to_columns(source, target):
+        send_sem, recv_sem = send_sems.take(), recv_sems.take()
 
         def one(step, carry):
             there = (c + step) % 32
@@ -111,7 +112,7 @@
             ).start()
             return carry
 
-        lax.fori_loop(*steps, one, 0)
+        lax.fori_loop(1, 32, one, 0)
         return send_sem, recv_sem
 
     def bulk(sources, target, sems):
@@ -143,7 +144,7 @@
         two_up.wait_recv()
         two_down.wait_recv()
         value = core[group, y] + twice[group, 0] + twice[group, 1]
-        home[:, group] = value.reshape(32, 8, 128)
+        home[group] = value.reshape(32, 8, 128)
 
     def over_rows(everyone):
         below, above, beyond = down * 2 + k, up * 2 + k, over * 2 + k
@@ -166,17 +167,15 @@
         for copy in across:
             copy.wait_recv()
 
-    def share_rows(everyone, home, pieces=1):
-        everyone[r, c] = home[c]
-        sems = None
-        for piece in range(pieces):
-            steps = (1 + 31 * piece // pieces, 1 + 31 * (piece + 1) // pieces)
-            sems = to_columns(lambda there: home.at[there], lambda here: everyone.at[r, here], sems, steps)
-            yield
-        both = bulk(home.at[pl.ds(0, 31)], everyone.at[r, pl.ds(0, 31)], sems)
+    def exchange(everyone, home, tile):
+        everyone[tile, r, c] = home[tile, c]
+        return to_columns(lambda there: home.at[tile, there], lambda here: everyone.at[tile, r, here])
+
+    def share(everyone, home, tile, sems):
+        both = bulk(home.at[tile, pl.ds(0, 31)], everyone.at[tile, r, pl.ds(0, 31)], sems)
         both.wait_recv()
         pending.append(both)
-        yield from over_rows(everyone)
+        yield from over_rows(everyone.at[tile])
 
     def ring(size, me, device, chunk):
         ahead, behind = (me + 1) % size, (me + size - 1) % size
@@ -203,31 +202,32 @@
         for generator in generators:
             yield from generator()
 
-    def run_together(generators, beside):
+    def run_together(generators, beside=()):
         live = list(generators)
         while live:
             for generator in list(live):
                 if next(generator, "end") == "end":
                     live.remove(generator)
-            next(beside, None)
-
-    row_of = lax.broadcasted_iota(jnp.int32, (256, 256), 0)
-    col_of = lax.broadcasted_iota(jnp.int32, (256, 256), 1) + r * 256
+            for generator in beside:
+                next(generator, None)
+
+    row_of = lax.broadcasted_iota(jnp.int32, (64, 256), 0)
+    col_of = lax.broadcasted_iota(jnp.int32, (64, 256), 1) + r * 256
 
     def split_d(order):
         sup = d_order[order]
         d_loads[order].wait()
 
         def one(piece, total):
-            rows = pl.ds(pl.multiple_of(piece * 256, 256), 256)
-            value = jnp.where(row_of + piece * 256 >= col_of, d_raw[order % 3, rows, :], 0.0)
+            rows = pl.ds(pl.multiple_of(piece * 64, 64), 64)
+            value = jnp.where(row_of + piece * 64 >= col_of, d_raw[order % 3, rows, :], 0.0)
             high, low = halves(value)
             d_high[sup, rows, :] = high
             d_low[sup, rows, :] = low
-            return total + jnp.sum(value * value, axis=0, keepdims=True)
-
-        total = lax.fori_loop(0, 8, one, jnp.zeros((1, 256), F32))
-        sums[sup, :] = total[0]
+            return total + jnp.sum((value * value).reshape(8, 8, 256), axis=0)
+
+        total = lax.fori_loop(0, 32, one, jnp.zeros((8, 256), F32), unroll=2)
+        sums[sup, :] = jnp.sum(total, axis=0)
         if order + 3 < NS:
             d_loads.append(load_d(order + 3))
 
@@ -237,8 +237,9 @@
     row_lane = lax.broadcasted_iota(jnp.int32, (64, 256), 1)
 
     def multiply(part, group, slots):
-        nothing = jnp.zeros((64, 256), BF16)
-        terms = []
+        nothing = jnp.zeros((64, 256), F32)
+        lane = lax.broadcasted_iota(jnp.int32, (256, 256), 1)
+        targets, weights = [], []
         for side, slot in enumerate(slots):
             if slot is None:
                 continue
@@ -249,18 +250,24 @@
             upper_mark = jnp.where(valid, marks[sup, 0, at], 0).astype(F32)
             lower_mark = jnp.where(valid, marks[sup, 1, at], 0).astype(F32)
             block = block_buf[at, sup] * jnp.where(row_lane < 128, upper_mark, lower_mark)
-            high, low = halves(block)
-            if side == 0:
-                both, one = [high, nothing, low, nothing], [high, nothing, nothing, nothing]
-            else:
-                both, one = [nothing, high, nothing, low], [nothing, high, nothing, nothing]
-            terms.append((at, jnp.concatenate(both, axis=0), jnp.concatenate(one, axis=0)))
-        for piece in range(8):
-            rows = pl.ds(piece * 256, 256)
-            total = jnp.zeros((256, 256), F32)
-            for at, both, one in terms:
-                total = total + mm(d_high[at, rows, :], both, NT) + mm(d_low[at, rows, :], one, NT)
-            part[group, piece // 2, piece % 2] = total[:, :128] + total[:, 128:]
+            high = block.astype(BF16).astype(F32)
+            low = block - high
+            rows = [high, nothing, low, nothing] if side == 0 else [nothing, high, nothing, low]
+            both = jnp.concatenate(rows, axis=0).T
+            targets.append(at)
+            weights += [both.astype(BF16), jnp.where(lane < 128, both, 0.0).astype(BF16)]
+        right = jnp.concatenate(weights, axis=0)
+
+        def one(piece, carry):
+            rows = pl.ds(pl.multiple_of(piece * 512, 512), 512)
+            left = [d_ref[at, rows, :] for at in targets for d_ref in (d_high, d_low)]
+            total = mm(jnp.concatenate(left, axis=1), right)
+            value = total[:, :128] + total[:, 128:]
+            part[group, piece, 0] = value[0:256]
+            part[group, piece, 1] = value[256:512]
+            return carry
+
+        lax.fori_loop(0, 4, one, 0)
 
     sums1 = [reduce_rows(part1, core1, once1, twice1, home1, group) for group in range(3)]
     sums2 = [reduce_rows(part2, core2, once2, twice2, home2, group) for group in range(2)]
@@ -273,28 +280,40 @@
     next(sums1[0])
     post_all[c] = post_rows[...]
     post_sems = to_columns(lambda there: post_rows, lambda here: post_all.at[here])
-    split_d(1)
-    next(sums1[0])
-    split_d(2)
-    multiply(part1, 1, FIRST[1])
-    next(sums1[1])
-    next(sums1[0])
-    split_d(3)
-    next(sums1[1])
-    split_d(4)
-    multiply(part1, 2, FIRST[2])
-    next(sums1[2])
-    next(sums1[0], None)
-    next(sums1[1])
-    next(sums1[2])
-    multiply(part2, 0, SECOND[0])
-    next(sums1[1], None)
-    next(sums1[2])
-    multiply(part2, 1, SECOND[1])
-    next(sums2[0])
-    next(sums2[1])
-    split_d(5)
-    next(sums1[2], None)
+    if early:
+        split_d(1)
+        next(sums1[0])
+        split_d(2)
+        multiply(part1, 1, FIRST[1])
+        next(sums1[1])
+        next(sums1[0])
+        split_d(3)
+        next(sums1[0], None)
+        moved1 = [None] * 3
+    else:
+        split_d(1)
+        next(sums1[0])
+        split_d(2)
+        multiply(part1, 1, FIRST[1])
+        next(sums1[1])
+        next(sums1[0])
+        split_d(3)
+        next(sums1[1])
+        split_d(4)
+        multiply(part1, 2, FIRST[2])
+        next(sums1[2])
+        next(sums1[0], None)
+        moved1 = [exchange(all1, home1, 0)]
+        next(sums1[1])
+        next(sums1[2])
+        multiply(part2, 0, SECOND[0])
+        next(sums2[0])
+        next(sums1[1], None)
+        moved1.append(exchange(all1, home1, 1))
+        next(sums1[2])
+        multiply(part2, 1, SECOND[1])
+        next(sums2[1])
+        next(sums1[2], None)
 
     flags = inner_flags(parent)
     picks = []
@@ -304,20 +323,19 @@
         before = before + flags[sup]
     where_of = {4: (0, 0), 2: (1, 0), 3: (1, 1), 1: (2, 1)}
     low_lanes = lax.broadcasted_iota(jnp.int32, (256, 128), 1) < 64
-    firsts = [home1[:, tile].reshape(256, 128) for tile in range(3)]
-    chosen = []
-    for place in range(width):
-        sides = [jnp.zeros((256, 128), F32), jnp.zeros((256, 128), F32)]
-        for sup, weight in picks:
-            tile, side = where_of[sup]
-            sides[side] = sides[side] + firsts[tile] * weight[place].astype(F32)
-        chosen.append(sides)
     rolled = lambda value: pltpu.roll(value, 64, 1)
-    if width == 1:
-        lo, hi = chosen[0]
-        in_low = jnp.where(low_lanes, lo + rolled(hi), 0.0)
-        spread[z, x] = jnp.where(low_lanes[0:128], in_low[0:128], rolled(in_low[128:256]))
+    if early:
+        value = home1[0].reshape(256, 128)
+        spread[z, x] = jnp.where(low_lanes[0:128], value[0:128], rolled(value[128:256]))
     else:
+        firsts = [home1[tile].reshape(256, 128) for tile in range(3)]
+        chosen = []
+        for place in range(2):
+            sides = [jnp.zeros((256, 128), F32), jnp.zeros((256, 128), F32)]
+            for sup, weight in picks:
+                tile, side = where_of[sup]
+                sides[side] = sides[side] + firsts[tile] * weight[place].astype(F32)
+            chosen.append(sides)
         lo = chosen[0][0] + rolled(chosen[0][1])
         hi = rolled(chosen[1][0]) + chosen[1][1]
         spread[z, x] = jnp.where(low_lanes, lo, hi)
@@ -336,9 +354,9 @@
         lambda: ring(8, z, on_z, lambda i, q: spread.at[i, :, quarter_of(2 + q)]),
     )
 
-    def up_copies():
-        all_up[r] = home1[:, 1:3]
-        yield from over_rows(all_up)
+    def up_copies(tile):
+        all_up[tile, r] = home1[1 + tile]
+        yield from over_rows(all_up.at[tile])
 
     pair_of = (lax.broadcasted_iota(jnp.int32, (256, 128), 0) % 8) // 2
 
@@ -350,7 +368,7 @@
     right_sum = [jnp.zeros((256, 128), F32)]
 
     def minus_post(home, group, slots):
-        parts = halves(home[:, group].reshape(256, 128))
+        parts = halves(home[group].reshape(256, 128))
         for slot in slots:
             if slot is None:
                 continue
@@ -359,7 +377,10 @@
             value = mm3((post_high[at], post_low[at]), parts)
             right_sum[0] = right_sum[0] - placed(sup, value)
 
-    def right_sides():
+    def right_sides(rounds):
+        for _ in range(rounds):
+            yield
+        split_d(5)
         yield
         post_both = bulk(post_all.at[pl.ds(0, 31)], post_all.at[pl.ds(0, 31)], post_sems)
         post_both.wait_recv()
@@ -381,11 +402,59 @@
         for group in range(3):
             minus_post(home1, group, FIRST[group])
 
-    share1 = share_rows(all1, home1, 4)
-    run_together((order_a, order_b, sums2[0], sums2[1], up_copies(), right_sides()), share1)
-
-    for pair in range(16):
-        cols = pl.ds(pair * 128, 128)
+    def last_exchange():
+        yield
+        yield
+        moved1.append(exchange(all1, home1, 2))
+
+    def first_copies(rounds):
+        for _ in range(rounds):
+            yield
+        yield from share(all1, home1, 0, moved1[0])
+        yield from share(all1, home1, 1, moved1[1])
+
+    def last_copies():
+        yield from share(all1, home1, 2, moved1[2])
+
+    def chain_one():
+        yield from sums1[1]
+        moved1[1] = exchange(all1, home1, 1)
+        yield from up_copies(0)
+
+    def chain_two():
+        split_d(4)
+        multiply(part1, 2, FIRST[2])
+        yield from sums1[2]
+        moved1[2] = exchange(all1, home1, 2)
+        yield from up_copies(1)
+
+    def chain_three():
+        yield
+        moved1[0] = exchange(all1, home1, 0)
+        multiply(part2, 0, SECOND[0])
+        yield from sums2[0]
+
+    def chain_four():
+        yield
+        yield
+        multiply(part2, 1, SECOND[1])
+        yield from sums2[1]
+
+    if early:
+        beside = [first_copies(7)]
+        run_together(
+            (order_a, order_b, chain_one(), chain_two(), chain_three(), chain_four(), right_sides(4)),
+            beside,
+        )
+    else:
+        beside = [first_copies(3)]
+        run_together(
+            (order_a, order_b, sums2[0], sums2[1], up_copies(0), up_copies(1), last_exchange(), right_sides(0)),
+            beside,
+        )
+
+    def merge(pair, carry):
+        cols = pl.ds(pl.multiple_of(pair * 128, 128), 128)
         even = spread[pair // 2, 2 * (pair % 2)]
         odd = spread[pair // 2, 2 * (pair % 2) + 1]
         wide = low_lanes[0:size]
@@ -397,6 +466,9 @@
             rows = pl.ds(side * size, size)
             h_high[rows, cols] = high
             h_low[rows, cols] = low
+        return carry
+
+    lax.fori_loop(0, 16, merge, 0)
     lane_256 = lax.broadcasted_iota(jnp.int32, (1, 256), 1)
     through = jnp.zeros((256, 256), F32)
     for place in range(width):
@@ -409,26 +481,29 @@
             keep = keep + jnp.where(lane_256 // 64 == at, chosen_here.astype(F32), 0.0)
         for row_block in range(8):
             right = jnp.concatenate(
-                [all_up[row_block, :, tile].reshape(256, 128) for tile in range(2)], axis=1
+                [all_up[tile, row_block].reshape(256, 128) for tile in range(2)], axis=1
             )
             cols = pl.ds(row_block * 256, 256)
             rows = pl.ds(place * 256, 256)
             through = through + mm3((h_high[rows, cols], h_low[rows, cols]), halves(right * keep))
+    moved2 = []
     for group in range(2):
-        value = home2[:, group].reshape(256, 128) - through[:, group * 128 : group * 128 + 128]
-        home2[:, group] = value.reshape(32, 8, 128)
+        value = home2[group].reshape(256, 128) - through[:, group * 128 : group * 128 + 128]
+        home2[group] = value.reshape(32, 8, 128)
+        moved2.append(exchange(all2, home2, group))
     for group in range(2):
         minus_post(home2, group, SECOND[group])
-    home2[:, 2] = right_sum[0].reshape(32, 8, 128)
+    home2[2] = right_sum[0].reshape(32, 8, 128)
+    moved2.append(exchange(all2, home2, 2))
 
     lane64 = low_lanes[0:64]
     lane8 = low_lanes[0:8]
 
     def gather_left(everyone, group):
-        for pair in range(16):
-            even = everyone[:, 2 * pair, group].reshape(64, 128)
-            odd = everyone[:, 2 * pair + 1, group].reshape(64, 128)
-            cols = pl.ds(pair * 128, 128)
+        def one(pair, carry):
+            even = everyone[group, :, 2 * pair].reshape(64, 128)
+            odd = everyone[group, :, 2 * pair + 1].reshape(64, 128)
+            cols = pl.ds(pl.multiple_of(pair * 128, 128), 128)
             for side, value in (
                 (0, jnp.where(lane64, even, rolled(odd))),
                 (1, jnp.where(lane64, rolled(even), odd)),
@@ -436,11 +511,14 @@
                 high, low = halves(value)
                 l_high[side, 0:64, cols] = high
                 l_low[side, 0:64, cols] = low
+            return carry
+
+        lax.fori_loop(0, 16, one, 0, unroll=2)
 
     def gather_sums(everyone, group):
         for pair in range(16):
-            even = jnp.sum(everyone[:, 2 * pair, group], axis=0)
-            odd = jnp.sum(everyone[:, 2 * pair + 1, group], axis=0)
+            even = jnp.sum(everyone[group, :, 2 * pair], axis=0)
+            odd = jnp.sum(everyone[group, :, 2 * pair + 1], axis=0)
             cols = pl.ds(pair * 128, 128)
             blank = jnp.zeros((8, 128), F32)
             for side, value in (
@@ -474,17 +552,10 @@
             if with_sums:
                 put_mean(slot[0], value[64:80])
 
-    share2 = share_rows(all2, home2)
-    next(share2)
-    for _ in share1:
-        pass
-    products(all1, 0, FIRST[0], False)
-    next(share2)
-    products(all1, 1, FIRST[1], False)
-    next(share2)
-    products(all1, 2, FIRST[2], False)
-    next(share2)
-    next(share2, None)
+    share2 = [share(all2, home2, tile, moved2[tile]) for tile in range(3)]
+    run_together(beside + [last_copies()] + share2)
+    for tile in range(3):
+        products(all1, tile, FIRST[tile], False)
     gather_sums(all2, 2)
     for group in range(2):
         products(all2, group, SECOND[group], True)
@@ -511,12 +582,13 @@
         pending.pop().wait_send()
 
 
-def sweep(width, parent, marks, blocks, diag_inv, post):
+def sweep(early, parent, marks, blocks, diag_inv, post):
+    width = 1 if early else 2
     any_ = pl.BlockSpec(memory_space=pl.ANY)
     vmem = pl.BlockSpec(memory_space=pltpu.VMEM)
     smem = pl.BlockSpec(memory_space=pltpu.SMEM)
     return pl.pallas_call(
-        functools.partial(sweep_kernel, width),
+        functools.partial(sweep_kernel, early),
         out_shape=(jax.ShapeDtypeStruct((NS, 2, 256), F32), jax.ShapeDtypeStruct((NS, 256), F32)),
         in_specs=[smem, smem, any_, any_, vmem],
         out_specs=(vmem, vmem),
@@ -529,11 +601,11 @@
             pltpu.VMEM((2, 2, 128, 128), F32),
             pltpu.VMEM((3, 2, 256, 128), F32),
             pltpu.VMEM((2, 2, 256, 128), F32),
-            pltpu.VMEM((32, 3, 8, 128), F32),
-            pltpu.VMEM((32, 3, 8, 128), F32),
-            pltpu.VMEM((8, 32, 3, 8, 128), F32),
-            pltpu.VMEM((8, 32, 3, 8, 128), F32),
-            pltpu.VMEM((8, 32, 2, 8, 128), F32),
+            pltpu.VMEM((3, 32, 8, 128), F32),
+            pltpu.VMEM((3, 32, 8, 128), F32),
+            pltpu.VMEM((3, 8, 32, 8, 128), F32),
+            pltpu.VMEM((3, 8, 32, 8, 128), F32),
+            pltpu.VMEM((2, 8, 32, 8, 128), F32),
             pltpu.VMEM((8, 4, width * 128, 128), F32),
             pltpu.VMEM((3, 2048, 256), F32),
             pltpu.VMEM((NS, 2048, 256), BF16),
@@ -553,12 +625,12 @@
             pltpu.VMEM((8, 256), F32),
             pltpu.VMEM((3, 8, 256), F32),
             pltpu.VMEM((8, 8, 256), F32),
-            pltpu.SemaphoreType.DMA((160,)),
-            pltpu.SemaphoreType.DMA((160,)),
+            pltpu.SemaphoreType.DMA((200,)),
+            pltpu.SemaphoreType.DMA((200,)),
             pltpu.SemaphoreType.DMA((7,)),
         ],
         compiler_params=pltpu.CompilerParams(
-            collective_id=width - 1, has_side_effects=True, vmem_limit_bytes=67_000_000
+            collective_id=int(early), has_side_effects=True, vmem_limit_bytes=67_000_000
         ),
         cost_estimate=pl.CostEstimate(flops=12_000_000_000, bytes_accessed=30_000_000, transcendentals=0),
     )(parent, marks, blocks, diag_inv, post)
@@ -567,7 +639,14 @@
 def body(factor, diag_inv, structure, parent, post):
     marks = jnp.transpose(structure, (0, 2, 1))
     blocks = jnp.transpose(factor, (0, 2, 3, 1))
-    mean, variance = sweep(2, parent, marks, blocks, diag_inv, jnp.transpose(post, (0, 2, 1)))
+    flags = inner_flags(parent)
+    only_four = (flags[4] == 1) & (flags[3] + flags[2] + flags[1] == 0)
+    mean, variance = lax.cond(
+        only_four,
+        functools.partial(sweep, True),
+        functools.partial(sweep, False),
+        parent, marks, blocks, diag_inv, jnp.transpose(post, (0, 2, 1)),
+    )
     return jnp.transpose(mean, (0, 2, 1)), variance
 
 

time: 130 us -> 126 us (0.969)
  Pallas kernels: 127 us -> 113 us
  between operations: 0.64 us -> 9.31 us
    pallas_call x1, Pallas kernels: 127 us -> 113 us  [sweep(): pl.pallas_call(functools.partial(sweep_kernel, early), out_shape=(jax.Sha...]
    slice x0 -> x1, local copies, waits for them, and re-layouts: none -> 1.51 us  [inner_flags(): parent[below] == sup]
    unnamed x2, local copies, waits for them, and re-layouts: 2.6 us -> 1.2 us
where the time goes in v4:
time: 126 us
  Pallas kernels  113 us (90%)
  between operations  9.31 us (7%)
  local copies, waits for them, and re-layouts  2.71 us (2%)
    pallas_call x1, Pallas kernels, sweep(): pl.pallas_call(functools.partial(sweep_kernel, early), out_shape=(jax.Sha...  113 us

profile of v4, /device:TPU:1, one launch (start us, length us, event | category | flops | bytes accessed | tf_op | source)
XLA Modules:
  0.0 125.7 jit_solution(11135755002405600751)
XLA Ops:
  0.6 1.5 %fusion = (s32[1]{0:T(128)}, s32[1]{0:T(128)}, s32[1]{0:T(128)}, s32[1]{0:T(128)}, s32[1]{0:T(128)}) fusion(s32[6]{0:T(128)} %param.10), kind=kLoop, calls=%fused_computation | loop fusion | bytes 40 | tf_op jit(solution)/shard_map/slice | solution.py:45
  10.8 113.7 %conditional.1 = ((f32[6,2,256]{2,1,0:T(2,128)S(1)}, f32[6,256]{1,0:T(8,128)S(1)})) conditional(s32[]{:T(128)} %bitcast, (s32[6]{0:T(128)}, s32[6,2,6]{2,1,0:T(2,128)}, f32[6,6,64,256]{3,2,1,0:T(8,128)}, f32[6,2048,256]{2,1,0:T(8,128)}, f32[6,2,256]{2,1,0:T(2,128)}) %tuple.30, (s32[6]{0:T(128)}, s32[6,2,6]{2,1,0:T(2,128)}, ...), branch_computations={%region_0.0_spmd, %region_1.0_spmd} | conditional | flops 12000000000 | bytes 30000008 | solution.py:644
  11.1 113.2 %branch_1_fun.1 = (f32[6,2,256]{2,1,0:T(2,128)S(1)}, f32[6,256]{1,0:T(8,128)S(1)}) custom-call(s32[6]{0:T(128)} %get-tuple-element.25.parent, s32[6,2,6]{2,1,0:T(2,128)} %get-tuple-element.26.marks, f32[6,6,64,256]{3,2,1,0:T(8,128)} %get-tuple-element.27.blocks, f32[6,2048,256]{2,1,0:T(8,128)} %get-tuple-element.28.diag_inv, f32[6,2,256]{2,1,0:T(2,128)} %get-tuple-element.29.post), custom_call_target="tpu_custom_call" | custom-call | flops 12000000000 | bytes 30000000 | tf_op jit(solution)/shard_map/cond/branch_1_fun/pallas_call | solution.py:590
  124.5 0.6 copy.13
  125.1 0.6 copy.14

commit v5 on v3

--- a/solution.py
+++ b/solution.py
@@ -29,7 +29,9 @@
 
 
 def mm3(left, right, dims=NN):
-    return mm(left[0], right[0], dims) + mm(left[1], right[0], dims) + mm(left[0], right[1], dims)
+    size = left[0].shape[0]
+    both = mm(jnp.concatenate(left, axis=0), right[0], dims)
+    return both[:size] + both[size:] + mm(left[0], right[1], dims)
 
 
 def ancestor_of(parent, sup, second):
@@ -100,8 +102,8 @@
     for device in ((up, k, z, x), (down, k, z, x), (y, 1 - k, z, x)):
         pl.semaphore_signal(barrier, inc=1, device_id=device, device_id_type=MESH)
 
-    def to_columns(source, target, sems=None, steps=(1, 32)):
-        send_sem, recv_sem = sems or (send_sems.take(), recv_sems.take())
+    def to_columns(source, target):
+        send_sem, recv_sem = send_sems.take(), recv_sems.take()
 
         def one(step, carry):
             there = (c + step) % 32
@@ -111,7 +113,7 @@
             ).start()
             return carry
 
-        lax.fori_loop(*steps, one, 0)
+        lax.fori_loop(1, 32, one, 0)
         return send_sem, recv_sem
 
     def bulk(sources, target, sems):
@@ -143,7 +145,7 @@
         two_up.wait_recv()
         two_down.wait_recv()
         value = core[group, y] + twice[group, 0] + twice[group, 1]
-        home[:, group] = value.reshape(32, 8, 128)
+        home[group] = value.reshape(32, 8, 128)
 
     def over_rows(everyone):
         below, above, beyond = down * 2 + k, up * 2 + k, over * 2 + k
@@ -166,17 +168,15 @@
         for copy in across:
             copy.wait_recv()
 
-    def share_rows(everyone, home, pieces=1):
-        everyone[r, c] = home[c]
-        sems = None
-        for piece in range(pieces):
-            steps = (1 + 31 * piece // pieces, 1 + 31 * (piece + 1) // pieces)
-            sems = to_columns(lambda there: home.at[there], lambda here: everyone.at[r, here], sems, steps)
-            yield
-        both = bulk(home.at[pl.ds(0, 31)], everyone.at[r, pl.ds(0, 31)], sems)
+    def exchange(everyone, home, tile):
+        everyone[tile, r, c] = home[tile, c]
+        return to_columns(lambda there: home.at[tile, there], lambda here: everyone.at[tile, r, here])
+
+    def share(everyone, home, tile, sems):
+        both = bulk(home.at[tile, pl.ds(0, 31)], everyone.at[tile, r, pl.ds(0, 31)], sems)
         both.wait_recv()
         pending.append(both)
-        yield from over_rows(everyone)
+        yield from over_rows(everyone.at[tile])
 
     def ring(size, me, device, chunk):
         ahead, behind = (me + 1) % size, (me + size - 1) % size
@@ -203,31 +203,32 @@
         for generator in generators:
             yield from generator()
 
-    def run_together(generators, beside):
+    def run_together(generators, beside=()):
         live = list(generators)
         while live:
             for generator in list(live):
                 if next(generator, "end") == "end":
                     live.remove(generator)
-            next(beside, None)
-
-    row_of = lax.broadcasted_iota(jnp.int32, (256, 256), 0)
-    col_of = lax.broadcasted_iota(jnp.int32, (256, 256), 1) + r * 256
+            for generator in beside:
+                next(generator, None)
+
+    row_of = lax.broadcasted_iota(jnp.int32, (64, 256), 0)
+    col_of = lax.broadcasted_iota(jnp.int32, (64, 256), 1) + r * 256
 
     def split_d(order):
         sup = d_order[order]
         d_loads[order].wait()
 
         def one(piece, total):
-            rows = pl.ds(pl.multiple_of(piece * 256, 256), 256)
-            value = jnp.where(row_of + piece * 256 >= col_of, d_raw[order % 3, rows, :], 0.0)
+            rows = pl.ds(pl.multiple_of(piece * 64, 64), 64)
+            value = jnp.where(row_of + piece * 64 >= col_of, d_raw[order % 3, rows, :], 0.0)
             high, low = halves(value)
             d_high[sup, rows, :] = high
             d_low[sup, rows, :] = low
-            return total + jnp.sum(value * value, axis=0, keepdims=True)
-
-        total = lax.fori_loop(0, 8, one, jnp.zeros((1, 256), F32))
-        sums[sup, :] = total[0]
+            return total + jnp.sum((value * value).reshape(8, 8, 256), axis=0)
+
+        total = lax.fori_loop(0, 32, one, jnp.zeros((8, 256), F32), unroll=2)
+        sums[sup, :] = jnp.sum(total, axis=0)
         if order + 3 < NS:
             d_loads.append(load_d(order + 3))
 
@@ -237,8 +238,9 @@
     row_lane = lax.broadcasted_iota(jnp.int32, (64, 256), 1)
 
     def multiply(part, group, slots):
-        nothing = jnp.zeros((64, 256), BF16)
-        terms = []
+        nothing = jnp.zeros((64, 256), F32)
+        lane = lax.broadcasted_iota(jnp.int32, (256, 256), 1)
+        targets, weights = [], []
         for side, slot in enumerate(slots):
             if slot is None:
                 continue
@@ -249,18 +251,20 @@
             upper_mark = jnp.where(valid, marks[sup, 0, at], 0).astype(F32)
             lower_mark = jnp.where(valid, marks[sup, 1, at], 0).astype(F32)
             block = block_buf[at, sup] * jnp.where(row_lane < 128, upper_mark, lower_mark)
-            high, low = halves(block)
-            if side == 0:
-                both, one = [high, nothing, low, nothing], [high, nothing, nothing, nothing]
-            else:
-                both, one = [nothing, high, nothing, low], [nothing, high, nothing, nothing]
-            terms.append((at, jnp.concatenate(both, axis=0), jnp.concatenate(one, axis=0)))
-        for piece in range(8):
-            rows = pl.ds(piece * 256, 256)
-            total = jnp.zeros((256, 256), F32)
-            for at, both, one in terms:
-                total = total + mm(d_high[at, rows, :], both, NT) + mm(d_low[at, rows, :], one, NT)
-            part[group, piece // 2, piece % 2] = total[:, :128] + total[:, 128:]
+            high = block.astype(BF16).astype(F32)
+            low = block - high
+            rows = [high, nothing, low, nothing] if side == 0 else [nothing, high, nothing, low]
+            both = jnp.concatenate(rows, axis=0).T
+            targets.append(at)
+            weights += [both.astype(BF16), jnp.where(lane < 128, both, 0.0).astype(BF16)]
+        right = jnp.concatenate(weights, axis=0)
+        for piece in range(4):
+            rows = pl.ds(piece * 512, 512)
+            left = [d_ref[at, rows, :] for at in targets for d_ref in (d_high, d_low)]
+            total = mm(jnp.concatenate(left, axis=1), right)
+            value = total[:, :128] + total[:, 128:]
+            part[group, piece, 0] = value[0:256]
+            part[group, piece, 1] = value[256:512]
 
     sums1 = [reduce_rows(part1, core1, once1, twice1, home1, group) for group in range(3)]
     sums2 = [reduce_rows(part2, core2, once2, twice2, home2, group) for group in range(2)]
@@ -285,15 +289,16 @@
     multiply(part1, 2, FIRST[2])
     next(sums1[2])
     next(sums1[0], None)
+    moved1 = [exchange(all1, home1, 0)]
     next(sums1[1])
     next(sums1[2])
     multiply(part2, 0, SECOND[0])
+    next(sums2[0])
     next(sums1[1], None)
+    moved1.append(exchange(all1, home1, 1))
     next(sums1[2])
     multiply(part2, 1, SECOND[1])
-    next(sums2[0])
     next(sums2[1])
-    split_d(5)
     next(sums1[2], None)
 
     flags = inner_flags(parent)
@@ -304,7 +309,7 @@
         before = before + flags[sup]
     where_of = {4: (0, 0), 2: (1, 0), 3: (1, 1), 1: (2, 1)}
     low_lanes = lax.broadcasted_iota(jnp.int32, (256, 128), 1) < 64
-    firsts = [home1[:, tile].reshape(256, 128) for tile in range(3)]
+    firsts = [home1[tile].reshape(256, 128) for tile in range(3)]
     chosen = []
     for place in range(width):
         sides = [jnp.zeros((256, 128), F32), jnp.zeros((256, 128), F32)]
@@ -336,9 +341,9 @@
         lambda: ring(8, z, on_z, lambda i, q: spread.at[i, :, quarter_of(2 + q)]),
     )
 
-    def up_copies():
-        all_up[r] = home1[:, 1:3]
-        yield from over_rows(all_up)
+    def up_copies(tile):
+        all_up[tile, r] = home1[1 + tile]
+        yield from over_rows(all_up.at[tile])
 
     pair_of = (lax.broadcasted_iota(jnp.int32, (256, 128), 0) % 8) // 2
 
@@ -350,7 +355,7 @@
     right_sum = [jnp.zeros((256, 128), F32)]
 
     def minus_post(home, group, slots):
-        parts = halves(home[:, group].reshape(256, 128))
+        parts = halves(home[group].reshape(256, 128))
         for slot in slots:
             if slot is None:
                 continue
@@ -360,6 +365,7 @@
             right_sum[0] = right_sum[0] - placed(sup, value)
 
     def right_sides():
+        split_d(5)
         yield
         post_both = bulk(post_all.at[pl.ds(0, 31)], post_all.at[pl.ds(0, 31)], post_sems)
         post_both.wait_recv()
@@ -381,8 +387,18 @@
         for group in range(3):
             minus_post(home1, group, FIRST[group])
 
-    share1 = share_rows(all1, home1, 4)
-    run_together((order_a, order_b, sums2[0], sums2[1], up_copies(), right_sides()), share1)
+    moved1.append(exchange(all1, home1, 2))
+
+    def later(rounds, tile):
+        for _ in range(rounds):
+            yield
+        yield from share(all1, home1, tile, moved1[tile])
+
+    beside = [later(3, 0), later(4, 1), later(4, 2)]
+    run_together(
+        (order_a, order_b, sums2[0], sums2[1], up_copies(0), up_copies(1), right_sides()),
+        beside,
+    )
 
     for pair in range(16):
         cols = pl.ds(pair * 128, 128)
@@ -409,25 +425,28 @@
             keep = keep + jnp.where(lane_256 // 64 == at, chosen_here.astype(F32), 0.0)
         for row_block in range(8):
             right = jnp.concatenate(
-                [all_up[row_block, :, tile].reshape(256, 128) for tile in range(2)], axis=1
+                [all_up[tile, row_block].reshape(256, 128) for tile in range(2)], axis=1
             )
             cols = pl.ds(row_block * 256, 256)
             rows = pl.ds(place * 256, 256)
             through = through + mm3((h_high[rows, cols], h_low[rows, cols]), halves(right * keep))
+    moved2 = []
     for group in range(2):
-        value = home2[:, group].reshape(256, 128) - through[:, group * 128 : group * 128 + 128]
-        home2[:, group] = value.reshape(32, 8, 128)
+        value = home2[group].reshape(256, 128) - through[:, group * 128 : group * 128 + 128]
+        home2[group] = value.reshape(32, 8, 128)
+        moved2.append(exchange(all2, home2, group))
     for group in range(2):
         minus_post(home2, group, SECOND[group])
-    home2[:, 2] = right_sum[0].reshape(32, 8, 128)
+    home2[2] = right_sum[0].reshape(32, 8, 128)
+    moved2.append(exchange(all2, home2, 2))
 
     lane64 = low_lanes[0:64]
     lane8 = low_lanes[0:8]
 
     def gather_left(everyone, group):
         for pair in range(16):
-            even = everyone[:, 2 * pair, group].reshape(64, 128)
-            odd = everyone[:, 2 * pair + 1, group].reshape(64, 128)
+            even = everyone[group, :, 2 * pair].reshape(64, 128)
+            odd = everyone[group, :, 2 * pair + 1].reshape(64, 128)
             cols = pl.ds(pair * 128, 128)
             for side, value in (
                 (0, jnp.where(lane64, even, rolled(odd))),
@@ -439,8 +458,8 @@
 
     def gather_sums(everyone, group):
         for pair in range(16):
-            even = jnp.sum(everyone[:, 2 * pair, group], axis=0)
-            odd = jnp.sum(everyone[:, 2 * pair + 1, group], axis=0)
+            even = jnp.sum(everyone[group, :, 2 * pair], axis=0)
+            odd = jnp.sum(everyone[group, :, 2 * pair + 1], axis=0)
             cols = pl.ds(pair * 128, 128)
             blank = jnp.zeros((8, 128), F32)
             for side, value in (
@@ -474,17 +493,10 @@
             if with_sums:
                 put_mean(slot[0], value[64:80])
 
-    share2 = share_rows(all2, home2)
-    next(share2)
-    for _ in share1:
-        pass
-    products(all1, 0, FIRST[0], False)
-    next(share2)
-    products(all1, 1, FIRST[1], False)
-    next(share2)
-    products(all1, 2, FIRST[2], False)
-    next(share2)
-    next(share2, None)
+    share2 = [share(all2, home2, tile, moved2[tile]) for tile in range(3)]
+    run_together(beside + share2)
+    for tile in range(3):
+        products(all1, tile, FIRST[tile], False)
     gather_sums(all2, 2)
     for group in range(2):
         products(all2, group, SECOND[group], True)
@@ -529,11 +541,11 @@
             pltpu.VMEM((2, 2, 128, 128), F32),
             pltpu.VMEM((3, 2, 256, 128), F32),
             pltpu.VMEM((2, 2, 256, 128), F32),
-            pltpu.VMEM((32, 3, 8, 128), F32),
-            pltpu.VMEM((32, 3, 8, 128), F32),
-            pltpu.VMEM((8, 32, 3, 8, 128), F32),
-            pltpu.VMEM((8, 32, 3, 8, 128), F32),
-            pltpu.VMEM((8, 32, 2, 8, 128), F32),
+            pltpu.VMEM((3, 32, 8, 128), F32),
+            pltpu.VMEM((3, 32, 8, 128), F32),
+            pltpu.VMEM((3, 8, 32, 8, 128), F32),
+            pltpu.VMEM((3, 8, 32, 8, 128), F32),
+            pltpu.VMEM((2, 8, 32, 8, 128), F32),
             pltpu.VMEM((8, 4, width * 128, 128), F32),
             pltpu.VMEM((3, 2048, 256), F32),
             pltpu.VMEM((NS, 2048, 256), BF16),
@@ -553,8 +565,8 @@
             pltpu.VMEM((8, 256), F32),
             pltpu.VMEM((3, 8, 256), F32),
             pltpu.VMEM((8, 8, 256), F32),
-            pltpu.SemaphoreType.DMA((160,)),
-            pltpu.SemaphoreType.DMA((160,)),
+            pltpu.SemaphoreType.DMA((200,)),
+            pltpu.SemaphoreType.DMA((200,)),
             pltpu.SemaphoreType.DMA((7,)),
         ],
         compiler_params=pltpu.CompilerParams(
@@ -564,10 +576,26 @@
     )(parent, marks, blocks, diag_inv, post)
 
 
+def count_kernel(parent, count):
+    count[0] = sum(inner_flags(parent).values())
+
+
+def inner_count(parent):
+    smem = pl.BlockSpec(memory_space=pltpu.SMEM)
+    return pl.pallas_call(
+        count_kernel, out_shape=jax.ShapeDtypeStruct((1,), jnp.int32), in_specs=[smem], out_specs=smem
+    )(parent)
+
+
 def body(factor, diag_inv, structure, parent, post):
     marks = jnp.transpose(structure, (0, 2, 1))
     blocks = jnp.transpose(factor, (0, 2, 3, 1))
-    mean, variance = sweep(2, parent, marks, blocks, diag_inv, jnp.transpose(post, (0, 2, 1)))
+    mean, variance = lax.cond(
+        inner_count(parent)[0] <= 1,
+        functools.partial(sweep, 1),
+        functools.partial(sweep, 2),
+        parent, marks, blocks, diag_inv, jnp.transpose(post, (0, 2, 1)),
+    )
     return jnp.transpose(mean, (0, 2, 1)), variance
 
 

time: 130 us -> 118 us (0.908)
  Pallas kernels: 127 us -> 114 us
  local copies, waits for them, and re-layouts: 2.6 us -> 1.2 us
    pallas_call x1, Pallas kernels: 127 us -> 113 us  [sweep(): pl.pallas_call(functools.partial(sweep_kernel, width), out_shape=(jax.Sha...]
    unnamed x2, local copies, waits for them, and re-layouts: 2.6 us -> 1.2 us
where the time goes in v5:
time: 118 us; the launch traced here: 117 us
  Pallas kernels  114 us (97%)
  between operations  1.29 us (1%)
  local copies, waits for them, and re-layouts  1.2 us (1%)
    pallas_call x1, Pallas kernels, sweep(): pl.pallas_call(functools.partial(sweep_kernel, width), out_shape=(jax.Sha...  113 us

profile of v5, /device:TPU:1, one launch (start us, length us, event | category | flops | bytes accessed | tf_op | source)
XLA Modules:
  0.0 117.5 jit_solution(789845057035316012)
XLA Ops:
  0.6 1.2 %shard_map.68 = s32[1]{0:T(128)} custom-call(s32[6]{0:T(128)} %parent.1), custom_call_target="tpu_custom_call" | custom-call | tf_op jit(solution)/shard_map/pallas_call | solution.py:585
  2.5 113.8 %conditional.1 = ((f32[6,2,256]{2,1,0:T(2,128)S(1)}, f32[6,256]{1,0:T(8,128)S(1)})) conditional(s32[]{:T(128)} %bitcast, (s32[6]{0:T(128)}, s32[6,2,6]{2,1,0:T(2,128)}, f32[6,6,64,256]{3,2,1,0:T(8,128)}, f32[6,2048,256]{2,1,0:T(8,128)}, f32[6,2,256]{2,1,0:T(2,128)}) %tuple.26, (s32[6]{0:T(128)}, s32[6,2,6]{2,1,0:T(2,128)}, ...), branch_computations={%region_0.0_spmd, %region_1.0_spmd} | conditional | flops 12000000000 | bytes 30000008 | solution.py:593
  2.7 113.3 %branch_1_fun.1 = (f32[6,2,256]{2,1,0:T(2,128)S(1)}, f32[6,256]{1,0:T(8,128)S(1)}) custom-call(s32[6]{0:T(128)} %get-tuple-element.25.parent, s32[6,2,6]{2,1,0:T(2,128)} %get-tuple-element.26.marks, f32[6,6,64,256]{3,2,1,0:T(8,128)} %get-tuple-element.27.blocks, f32[6,2048,256]{2,1,0:T(8,128)} %get-tuple-element.28.diag_inv, f32[6,2,256]{2,1,0:T(2,128)} %get-tuple-element.29.post), custom_call_target="tpu_custom_call" | custom-call | flops 12000000000 | bytes 30000000 | tf_op jit(solution)/shard_map/cond/branch_1_fun/pallas_call | solution.py:530
  116.3 0.6 copy.13
  116.9 0.6 copy.14
